TPU v7x, 256 devices: a whole 4x4x8 slice. The times are simulated.
256 devices in a mesh: blk: 64 (over x_lo, y, z), mp: 4 (over x_hi, core).
Axes of the slice: x: 4 (x_hi: 2, x_lo: 2; x = x_hi * 2 + x_lo), y: 4, z: 8, core: 2. Of those that a mesh axis runs over, the one named last changes fastest.
Arguments:
- tokens: bfloat16 [8192, 2048], P('blk', 'mp'), may hold values from -16 to 16
- grad_out: bfloat16 [8192, 2048], P('blk', 'mp'), may hold values from -0.29882812 to 0.29882812
- w_gate: bfloat16 [2048, 2560], P(None, 'mp'), may hold values from -0.125 to 0.125
- w_lin: bfloat16 [2048, 2560], P(None, 'mp'), may hold values from -0.125 to 0.125
- w_out_t: bfloat16 [2048, 2560], P(None, 'mp'), may hold values from -0.125 to 0.125
- code: float32 [64, 5], P('blk'), may hold values from 0.5 to 2
- decode: float32 [64], P('blk'), may hold values from 0.05 to 0.2
- stragglers: int32 [4], replicated, may hold values from 0 to 63, as said below
Outputs:
- grads: float32 [2048, 3, 2560], P('blk', None, 'mp')
Inputs may be any that keep to these rules, and one draw needn't show every extreme that they name: `stragglers`: 4 distinct worker indices; worker 0 and worker 64 - 1 are always among them.
All inputs are finite; a program needn't handle non-finite values.
Results may differ from a plain program's by a relative error of at most 0.0042.
Values may be sent and summed in bfloat16 or wider, within the bound.
A program may use at most 128 MiB of HBM per device.

v0:
```python
from functools import partial

import jax
import jax.numpy as jnp
from jax import lax
from jax.sharding import PartitionSpec as P


def from_behind(block, axis, distance):
    devices = range(lax.axis_size(axis))
    route = [((i - distance) % len(devices), i) for i in devices]
    return lax.ppermute(block, axis, route)


def sent_to_all(shard, axis):
    copies = jnp.broadcast_to(shard, (lax.axis_size(axis), *shard.shape))
    return lax.all_to_all(copies, axis, split_axis=0, concat_axis=0, tiled=True)


def laid_out(blocks, dim):
    blocks = jnp.moveaxis(blocks, 0, dim)
    dims = blocks.shape
    return blocks.reshape(*dims[:dim], dims[dim] * dims[dim + 1], *dims[dim + 2 :])


def gathered_copies(shard, axis, dim):
    blocks = sent_to_all(shard, axis)
    return laid_out(blocks, dim)


def in_blocks(shard, dim, peers):
    before, after = (shard.shape[:dim], shard.shape[dim + 1 :])
    return jnp.moveaxis(shard.reshape(*before, peers, -1, *after), dim, 0)


def sent_and_summed(shard, axis, dim):
    peers = lax.axis_size(axis)
    blocks = lax.all_to_all(in_blocks(shard, dim, peers), axis, 0, 0, tiled=True)
    return jnp.sum(blocks.astype(jnp.float32), axis=0)


def local_grads(inputs, cotangent, w_gate, w_lin, w_out_t):
    gate_pre = jnp.dot(inputs, w_gate, preferred_element_type=jnp.float32)
    linear = jnp.dot(inputs, w_lin, preferred_element_type=jnp.float32)
    activated, pullback = jax.vjp(partial(jax.nn.gelu, approximate=True), gate_pre)
    hidden = (activated * linear).astype(jnp.bfloat16)
    hidden_grad = jnp.dot(cotangent, w_out_t, preferred_element_type=jnp.float32)
    d_gate = pullback(hidden_grad * linear)[0].astype(jnp.bfloat16)
    d_lin = (hidden_grad * activated).astype(jnp.bfloat16)
    return (jnp.concatenate([d_gate, d_lin], axis=1), hidden)


def shards(tokens, grad_out, w_gate, w_lin, w_out_t, code, decode, stragglers):
    device = lax.axis_index("blk")
    group_size = lax.axis_size("blk")
    slot_total = code.shape[1]
    part_rows = tokens.shape[0]
    is_alive = jnp.all(stragglers != device)
    own_decode = jnp.where(is_alive, decode[0], jnp.float32(0.0))
    token_pair = jnp.stack([tokens, grad_out])
    weighted_row = own_decode * code[0]
    total_weight = weighted_row[0]
    passed = weighted_row
    for slot in range(1, slot_total):
        passed = from_behind(passed, "blk", 1)
        total_weight = total_weight + passed[slot]
    coefficients = [total_weight]
    stacked = gathered_copies(token_pair, "mp", 2)[None]
    used_slots = len(coefficients)
    width = stacked.shape[-1]
    inputs_all = stacked[:, 0].reshape(used_slots * part_rows, width)
    cotangent_all = stacked[:, 1].reshape(used_slots * part_rows, width)
    right_side, hidden = local_grads(inputs_all, cotangent_all, w_gate, w_lin, w_out_t)
    local_width = hidden.shape[1]
    own_rows = width // group_size
    accumulated = jnp.zeros((width, 3 * local_width), jnp.float32)
    slot = 0
    lower = slot * part_rows
    product = jnp.concatenate(
        [
            jnp.dot(
                inputs_all.T,
                right_side[lower : lower + part_rows],
                preferred_element_type=jnp.float32,
            ),
            jnp.dot(
                cotangent_all.T,
                hidden[lower : lower + part_rows],
                preferred_element_type=jnp.float32,
            ),
        ],
        axis=1,
    )
    accumulated = accumulated + coefficients[slot] * product
    summed = sent_and_summed(accumulated.astype(jnp.bfloat16), "blk", 0)
    return summed.reshape(own_rows, 3, local_width)


def solution(mesh):
    in_specs = (
        P("blk", "mp"),
        P("blk", "mp"),
        P(None, "mp"),
        P(None, "mp"),
        P(None, "mp"),
        P("blk", None),
        P("blk"),
        P(),
    )
    out_specs = P("blk", None, "mp")
    return jax.shard_map(shards, mesh=mesh, in_specs=in_specs, out_specs=out_specs, check_vma=False)
```

profile of v0, /device:TPU:8, one launch (start us, length us, event | category | flops | bytes accessed | tf_op | source)
XLA Modules:
  0.0 235.0 jit_solution(6701647623635985856)
XLA Ops:
  0.0 1.1 pad_maximum_fusion
  1.1 0.2 copy.14
  1.3 1.2 broadcast_in_dim.3
  2.5 4.3 %all-to-all-start = ((bf16[4,2,128,512]{2,3,1,0:T(8,128)(2,1)}), bf16[4,2,128,512]{2,3,1,0:T(8,128)(2,1)}, u32[]{:S(2)}, u32[]{:S(2)}) async-start(bf16[4,2,128,512]{2,3,1,0:T(8,128)(2,1)} %broadcast_in_dim.3), calls=%async_computation | async-start | bytes 2097152 | tf_op jit(solution)/shard_map/all_to_all | solution.py:17
  7.4 1.3 compare_reduce_fusion
  9.4 0.7 fusion.34
  10.0 1.9 collective-permute-start
  11.9 0.7 broadcast_multiply_fusion
  12.6 4.7 %collective-permute-done = f32[5]{0:T(128)S(1)} collective-permute-done((f32[5]{0:T(128)S(1)}, f32[5]{0:T(128)S(1)}, u32[]{:S(2)}, u32[]{:S(2)}) %collective-permute-start) | collective-permute-done | bytes 52 | tf_op jit(solution)/shard_map/ppermute | solution.py:12
  17.3 0.6 slice.26
  18.6 0.1 collective-permute-start.1
  18.7 5.7 %collective-permute-done.1 = f32[5]{0:T(128)S(1)} collective-permute-done((f32[5]{0:T(128)S(1)}, f32[5]{0:T(128)S(1)}, u32[]{:S(2)}, u32[]{:S(2)}) %collective-permute-start.1) | collective-permute-done | bytes 52 | tf_op jit(solution)/shard_map/ppermute | solution.py:12
  24.3 0.6 slice.27
  25.6 0.1 collective-permute-start.2
  25.7 5.7 %collective-permute-done.2 = f32[5]{0:T(128)S(1)} collective-permute-done((f32[5]{0:T(128)S(1)}, f32[5]{0:T(128)S(1)}, u32[]{:S(2)}, u32[]{:S(2)}) %collective-permute-start.2) | collective-permute-done | bytes 52 | tf_op jit(solution)/shard_map/ppermute | solution.py:12
  31.3 0.6 slice.28
  32.6 0.1 collective-permute-start.3
  32.7 5.7 %collective-permute-done.3 = f32[5]{0:T(128)S(1)} collective-permute-done((f32[5]{0:T(128)S(1)}, f32[5]{0:T(128)S(1)}, u32[]{:S(2)}, u32[]{:S(2)}) %collective-permute-start.3) | collective-permute-done | bytes 52 | tf_op jit(solution)/shard_map/ppermute | solution.py:12
  38.3 0.6 slice.29
  39.6 0.0 all-to-all-done
  39.6 0.0 copy-start.1
  39.6 1.4 copy.15
  41.0 0.1 fusion.28
  41.1 2.3 fusion.3
  43.5 0.6 fusion.1
  44.1 0.8 fusion.13
  45.0 0.9 fusion.18
  45.8 1.5 fusion.14
  47.4 1.2 fusion
  48.6 184.6 %all_to_all.10 = bf16[64,32,1920]{2,1,0:T(8,128)(2,1)S(1)} all-to-all(bf16[64,32,1920]{2,1,0:T(8,128)(2,1)S(1)} %fusion), channel_id=1, replica_groups=mesh['blk'=64,'mp'=4] {'blk'}, dimensions={0} | all-to-all | bytes 15728640 | tf_op jit(solution)/shard_map/all_to_all | solution.py:38
  233.2 1.2 convert_reduce_fusion
  234.3 0.7 copy.19
  (3 shorter events, 0.0 us)
Async XLA Ops:
  0.0 44.1 %copy-start = (bf16[2048,640]{1,0:T(8,128)(2,1)S(1)}, bf16[2048,640]{1,0:T(8,128)(2,1)}, u32[]{:S(2)}) copy-start(bf16[2048,640]{1,0:T(8,128)(2,1)} %param.10) | copy-start | bytes 7864324
  2.5 37.1 %all-to-all-start = ((bf16[4,2,128,512]{2,3,1,0:T(8,128)(2,1)}), bf16[4,2,128,512]{2,3,1,0:T(8,128)(2,1)}, u32[]{:S(2)}, u32[]{:S(2)}) async-start(bf16[4,2,128,512]{2,3,1,0:T(8,128)(2,1)} %broadcast_in_dim.3), calls=%async_computation | async-start | bytes 2097152 | tf_op jit(solution)/shard_map/all_to_all | solution.py:17
  10.0 7.3 %collective-permute-start = (f32[5]{0:T(128)S(1)}, f32[5]{0:T(128)S(1)}, u32[]{:S(2)}, u32[]{:S(2)}) collective-permute-start(f32[5]{0:T(128)S(1)} %fusion.34), channel_id=1, source_target_pairs={{252,0},{0,4},{4,8},{8,12},{12,16},{16,20},{20,24},{24,28},{28,32}... | collective-permute-start | bytes 68 | tf_op jit(solution)/shard_map/ppermute | solution.py:12
  18.6 5.8 %collective-permute-start.1 = (f32[5]{0:T(128)S(1)}, f32[5]{0:T(128)S(1)}, u32[]{:S(2)}, u32[]{:S(2)}) collective-permute-start(f32[5]{0:T(128)S(1)} %collective-permute-done), channel_id=1, source_target_pairs={{252,0},{0,4},{4,8},{8,12},{12,16},{16,20},{20,24},{24,28},{28,32}... | collective-permute-start | bytes 68 | tf_op jit(solution)/shard_map/ppermute | solution.py:12
  25.6 5.8 %collective-permute-start.2 = (f32[5]{0:T(128)S(1)}, f32[5]{0:T(128)S(1)}, u32[]{:S(2)}, u32[]{:S(2)}) collective-permute-start(f32[5]{0:T(128)S(1)} %collective-permute-done.1), channel_id=1, source_target_pairs={{252,0},{0,4},{4,8},{8,12},{12,16},{16,20},{20,24},{24,28},{28,32}... | collective-permute-start | bytes 68 | tf_op jit(solution)/shard_map/ppermute | solution.py:12
  32.6 5.8 %collective-permute-start.3 = (f32[5]{0:T(128)S(1)}, f32[5]{0:T(128)S(1)}, u32[]{:S(2)}, u32[]{:S(2)}) collective-permute-start(f32[5]{0:T(128)S(1)} %collective-permute-done.2), channel_id=1, source_target_pairs={{252,0},{0,4},{4,8},{8,12},{12,16},{16,20},{20,24},{24,28},{28,32}... | collective-permute-start | bytes 68 | tf_op jit(solution)/shard_map/ppermute | solution.py:12
  39.6 3.9 %copy-start.1 = (bf16[2048,640]{1,0:T(8,128)(2,1)S(1)}, bf16[2048,640]{1,0:T(8,128)(2,1)}, u32[]{:S(2)}) copy-start(bf16[2048,640]{1,0:T(8,128)(2,1)} %param.12) | copy-start | bytes 7864324
where the time goes:
time: 238 us; the launch traced here: 235 us
  blocking collectives  185 us (78%)
  waiting for transfers between devices  21.7 us (9%)
  starting transfers between devices  6.46 us (3%)
  matrix products  6.19 us (3%)
  other arithmetic  6.13 us (3%)
  local copies, waits for them, and re-layouts  5.88 us (2%)
  between operations  4.07 us (2%)
    all_to_all x1, blocking collectives, sent_and_summed(): lax.all_to_all(in_blocks(shard, dim, peers), axis, 0, 0, tiled=True)  185 us
    ppermute x4, waiting for transfers between devices, from_behind(): return lax.ppermute(block, axis, route)  21.7 us
  transfers between devices with their start and end apart: 5, of which 4 were waited for; matrix products, arithmetic and copies ran while one was open for 2% of the time, Pallas kernels for 0%

commit v1 on v0

v1 whole, which is shorter than its diff:
```python
import functools

import jax
import jax.numpy as jnp
from jax import lax
from jax.experimental import pallas as pl
from jax.experimental.pallas import tpu as pltpu
from jax.sharding import PartitionSpec as P

MESH = pl.DeviceIdType.MESH
BF16 = jnp.bfloat16
F32 = jnp.float32

NX, NY, NZ = 4, 4, 8
SIZE = {"y": NY, "z": NZ}
ROWS = 128
WIDTH = 512
HID = 640
OWN = 32
WLANES = 256

STREAMS = (
    ("z", "y", 0, 256, 1),
    ("z", "y", 256, 256, -1),
    ("z", "y", 512, 256, 1),
    ("z", "y", 768, 128, -1),
    ("y", "z", 896, 256, 1),
    ("y", "z", 1152, 256, -1),
    ("y", "z", 1408, 256, 1),
    ("y", "z", 1664, 256, -1),
)
SPLIT = 896


def steps_of(n, sigma):
    half = n // 2
    steps = []
    for t in range(1, half + 1):
        step = [(sigma, half + 1 - t, t - 1, t - 2 if t > 1 else None)]
        if t < half:
            step.append((-sigma, half - t, half + t - 1, half + t - 2 if t > 1 else None))
        steps.append(step)
    return steps


def last_slots(n):
    return (n // 2 - 1, n - 2)


def gelu_parts(u):
    c = 0.7978845608028654
    t = jnp.tanh(c * (u + 0.044715 * (u * u * u)))
    half = 0.5 * (1.0 + t)
    act = u * half
    slope = half + 0.5 * u * (1.0 - t * t) * (c * (1.0 + 3.0 * 0.044715 * (u * u)))
    return act, slope


def kernel(
    tok, gout, w_gate, w_lin, w_out, code, decode, strag,
    out,
    gath, wg, wl, wo, acc_g, acc_l, acc_h, dmat, xt, yt, prod, vec, wrecv, wpair, *rest,
):
    n_streams = len(STREAMS)
    snd1, rcv1 = rest[:n_streams], rest[n_streams : 2 * n_streams]
    snd2, rcv2 = rest[2 * n_streams : 3 * n_streams], rest[3 * n_streams : 4 * n_streams]
    mid = rest[4 * n_streams : 5 * n_streams]
    (loc_sem, gs_sem, gr_sem, ds_sem, dr_sem, ws_sem, wr_sem, s1, r1, s2, r2) = rest[5 * n_streams :]

    b = lax.axis_index("blk")
    m = lax.axis_index("mp")
    x_lo, yz = lax.div(b, NY * NZ), lax.rem(b, NY * NZ)
    y, z = lax.div(yz, NZ), lax.rem(yz, NZ)
    x_hi, core = lax.div(m, 2), lax.rem(m, 2)
    x = 2 * x_hi + x_lo
    me = {"y": y, "z": z}

    def device(px, py, pz, pc):
        return (lax.rem(px, 2) * (NY * NZ) + py * NZ + pz, lax.div(px, 2) * 2 + pc)

    def x_shift(d):
        return lax.rem(x + d + NX, NX)

    def ring_device(axis, d):
        q = lax.rem(me[axis] + d + SIZE[axis], SIZE[axis])
        return device(x, q, z, core) if axis == "y" else device(x, y, q, core)

    right, left = device(x_shift(1), y, z, core), device(x_shift(-1), y, z, core)
    sibling = device(x, y, z, 1 - core)
    pair = (lax.rem(b + NY * NZ, 2 * NY * NZ), m)

    mine = pl.ds(pl.multiple_of(x_lo * ROWS, ROWS), ROWS)
    load_x = pltpu.make_async_copy(tok, gath.at[m, 0, mine, :], loc_sem.at[0])
    load_y = pltpu.make_async_copy(gout, gath.at[m, 1, mine, :], loc_sem.at[1])
    load_x.start()
    load_y.start()
    loads_w = [
        pltpu.make_async_copy(src, dst, loc_sem.at[2 + i])
        for i, (src, dst) in enumerate(((w_gate, wg), (w_lin, wl), (w_out, wo)))
    ]
    for load in loads_w:
        load.start()

    barrier = pltpu.get_barrier_semaphore()
    partners = [right, left, sibling]
    partners += [ring_device(axis, d) for axis in ("y", "z") for d in (1, -1)]
    partners += [(lax.rem(b + d + 64, 64), m) for d in (1, 2, 3, 4, -1, -2, -3, -4)]
    for partner in partners:
        pl.semaphore_signal(barrier, inc=1, device_id=partner, device_id_type=MESH)

    alive = (strag[0] != b) & (strag[1] != b) & (strag[2] != b) & (strag[3] != b)
    own_decode = jnp.where(alive, decode[0], 0.0)
    row_id = lax.broadcasted_iota(jnp.int32, (8, WLANES), 0)
    coeffs = jnp.zeros((8, WLANES), F32)
    for j in range(5):
        coeffs = jnp.where(row_id == j, own_decode * code[0, j], coeffs)
    vec[...] = coeffs
    pl.semaphore_wait(barrier, len(partners))

    def remote(src, dst, ss, rs, to):
        return pltpu.make_async_remote_copy(
            src_ref=src, dst_ref=dst, send_sem=ss, recv_sem=rs, device_id=to, device_id_type=MESH
        )

    pending = []

    def go(src, dst, ss, rs, to):
        copy = remote(src, dst, ss, rs, to)
        copy.start()
        pending.append(copy)
        return copy

    def slot(px, pc, kind):
        rows = pl.ds(pl.multiple_of(lax.rem(px, 2) * ROWS, ROWS), ROWS)
        return gath.at[lax.div(px, 2) * 2 + pc, kind, rows, :]

    own_slot = [slot(x, core, k) for k in (0, 1)]
    load_x.wait()
    from_left = [None, None]
    from_right = [None, None]
    from_left[0] = go(own_slot[0], own_slot[0], gs_sem.at[0], gr_sem.at[0], right)
    load_y.wait()
    from_right[1] = go(own_slot[1], own_slot[1], gs_sem.at[3], gr_sem.at[3], left)
    from_left[1] = go(own_slot[1], own_slot[1], gs_sem.at[1], gr_sem.at[1], right)
    from_right[0] = go(own_slot[0], own_slot[0], gs_sem.at[2], gr_sem.at[2], left)
    sib = {}

    def to_sibling(rel, kind):
        src = slot(x_shift(rel), core, kind)
        idx = (rel % 4) * 2 + kind
        sib[rel, kind] = go(src, src, ds_sem.at[idx], dr_sem.at[idx], sibling)

    to_sibling(0, 0)
    to_sibling(0, 1)
    wcopies = [
        go(vec, wrecv.at[j - 1], ws_sem.at[j - 1], wr_sem.at[j - 1], (lax.rem(b + j, 64), m)) for j in (1, 2, 3, 4)
    ]
    from_left[0].wait_recv()
    left_x = slot(x_shift(-1), core, 0)
    far_x = go(left_x, left_x, gs_sem.at[4], gr_sem.at[4], right)
    to_sibling(-1, 0)
    from_right[1].wait_recv()
    right_y = slot(x_shift(1), core, 1)
    far_y = go(right_y, right_y, gs_sem.at[5], gr_sem.at[5], left)
    to_sibling(1, 1)
    for copy in wcopies:
        copy.wait_recv()
    total = vec[0:1, :]
    for j in (1, 2, 3, 4):
        total = total + wrecv[j - 1, j : j + 1, :]
    wpair[x_lo] = jnp.broadcast_to(total, (8, WLANES))
    wswap = go(wpair.at[x_lo], wpair.at[x_lo], ws_sem.at[4], wr_sem.at[4], pair)
    from_left[1].wait_recv()
    to_sibling(-1, 1)
    from_right[0].wait_recv()
    to_sibling(1, 0)
    for load in loads_w:
        load.wait()
    for rel in (0, -1, 1):
        for kind in (0, 1):
            sib[rel, kind].wait_recv()

    def forward(mm, first):
        ks = pl.ds(pl.multiple_of(mm * WIDTH, WIDTH), WIDTH)
        for kind, w, acc in ((0, wg, acc_g), (0, wl, acc_l), (1, wo, acc_h)):
            part = jnp.dot(gath[mm, kind], w[ks, :], preferred_element_type=F32)
            acc[...] = part if first else acc[...] + part

    forward(2 * x_hi, True)
    forward(2 * x_hi + 1, False)
    far_x.wait_recv()
    to_sibling(2, 0)
    far_y.wait_recv()
    to_sibling(2, 1)
    forward(2 * (1 - x_hi) + core, False)
    sib[2, 0].wait_recv()
    sib[2, 1].wait_recv()
    forward(2 * (1 - x_hi) + 1 - core, False)
    for i in range(2):
        xt[pl.ds(i * WIDTH, WIDTH), :] = gath[2 * x_lo + i, 0].T
        yt[pl.ds(i * WIDTH, WIDTH), :] = gath[2 * x_lo + i, 1].T

    def elementwise(i, carry):
        rows = pl.ds(pl.multiple_of(i * 16, 16), 16)
        act, slope = gelu_parts(acc_g[rows, :])
        lin, dh = acc_l[rows, :], acc_h[rows, :]
        dmat[rows, 0:HID] = (dh * lin * slope).astype(BF16)
        dmat[rows, HID : 2 * HID] = (dh * act).astype(BF16)
        dmat[rows, 2 * HID :] = (act * lin).astype(BF16)
        return carry

    lax.fori_loop(0, 2 * ROWS // 16, elementwise, 0)
    wswap.wait_recv()
    weight = [wpair[i, 0:1, :] for i in (0, 1)]

    def products(yd, lower, upper):
        rows = pl.ds(pl.multiple_of(yd * (NZ * OWN), NZ * OWN), NZ * OWN)
        col = lower
        while col < upper:
            stop = min(upper, col + 256)
            if col < 2 * HID:
                stop = min(stop, 2 * HID)
            lhs = xt if col < 2 * HID else yt
            width = stop - col
            value = None
            for i in (0, 1):
                tokens = slice(i * ROWS, (i + 1) * ROWS)
                part = jnp.dot(lhs[rows, tokens], dmat[tokens, col:stop], preferred_element_type=F32)
                part = weight[i][:, :width] * part
                value = part if value is None else value + part
            prod[yd, :, :, col:stop] = value.reshape(NZ, OWN, width)
            col = stop

    def local1(s, d):
        axis, _, col, width, _ = STREAMS[s]
        cols = slice(col, col + width)
        return prod[:, d, :, cols] if axis == "z" else prod[d, :, :, cols]

    def run(s):
        axis1, axis2, col, width, sigma = STREAMS[s]
        for phase, axis, snd, rcv, ss, rs in ((1, axis1, snd1[s], rcv1[s], s1, r1), (2, axis2, snd2[s], rcv2[s], s2, r2)):
            n = SIZE[axis]
            local = functools.partial(local1, s) if phase == 1 else lambda d: mid[s][d]
            base = s * 8
            flying = {}
            for step in steps_of(n, sigma):
                for direction, distance, index, before in step:
                    yield (s, phase, "send", direction, distance)
                    dest = lax.rem(me[axis] + direction * distance + n, n)
                    value = local(dest)
                    if before is not None:
                        flying[before].wait_recv()
                        value = value + rcv[before].astype(F32)
                    snd[index] = value.astype(BF16)
                    flying[index] = go(
                        snd.at[index], rcv.at[index], ss.at[base + index], rs.at[base + index],
                        ring_device(axis, direction),
                    )
            yield (s, phase, "sum")
            value = local(me[axis])
            for index in last_slots(n):
                flying[index].wait_recv()
                value = value + rcv[index].astype(F32)
            if phase == 1:
                mid[s][...] = value
            else:
                out[:, col : col + width] = value

    runs = [run(s) for s in range(n_streams)]
    heads = [next(r) for r in runs]

    def advance(s, until):
        while heads[s] is not None and not until(heads[s]):
            heads[s] = next(runs[s], None)

    y_first = [s for s in range(n_streams) if STREAMS[s][0] == "y"]
    z_first = [s for s in range(n_streams) if STREAMS[s][0] == "z"]
    far = lax.rem(y + 2, NY)
    products(far, SPLIT, 3 * HID)
    for s in y_first[:2]:
        advance(s, lambda h: h[4] != 2)
    for d in range(NY):
        products(jnp.int32(d), 0, SPLIT)
    for s in z_first:
        advance(s, lambda h: h[4] != 4)
    products(lax.rem(y + 1, NY), SPLIT, 3 * HID)
    products(lax.rem(y + 3, NY), SPLIT, 3 * HID)
    for s in y_first[:2]:
        advance(s, lambda h: h[2] == "sum" or h[4] == 1 and h[3] == STREAMS[s][4])
    for s in z_first:
        advance(s, lambda h: h[2] == "sum" or h[4] <= 3 and h[3] == STREAMS[s][4])
    products(y, SPLIT, 3 * HID)
    order = []
    for _ in range(24):
        order += y_first + z_first
    for s in order:
        if heads[s] is not None:
            heads[s] = next(runs[s], None)
    assert all(h is None for h in heads)
    for copy in pending:
        copy.wait_send()


def shards(tokens, grad_out, w_gate, w_lin, w_out_t, code, decode, stragglers):
    n = len(STREAMS)
    scratch = [
        pltpu.VMEM((4, 2, 2 * ROWS, WIDTH), BF16),
        pltpu.VMEM((4 * WIDTH, HID), BF16),
        pltpu.VMEM((4 * WIDTH, HID), BF16),
        pltpu.VMEM((4 * WIDTH, HID), BF16),
        pltpu.VMEM((2 * ROWS, HID), F32),
        pltpu.VMEM((2 * ROWS, HID), F32),
        pltpu.VMEM((2 * ROWS, HID), F32),
        pltpu.VMEM((2 * ROWS, 3 * HID), BF16),
        pltpu.VMEM((2 * WIDTH, 2 * ROWS), BF16),
        pltpu.VMEM((2 * WIDTH, 2 * ROWS), BF16),
        pltpu.VMEM((NY, NZ, OWN, 3 * HID), F32),
        pltpu.VMEM((8, WLANES), F32),
        pltpu.VMEM((4, 8, WLANES), F32),
        pltpu.VMEM((2, 8, WLANES), F32),
    ]
    first = [pltpu.VMEM((SIZE[a] - 1, SIZE[c], OWN, w), BF16) for a, c, _, w, _ in STREAMS]
    second = [pltpu.VMEM((SIZE[c] - 1, OWN, w), BF16) for a, c, _, w, _ in STREAMS]
    scratch += first + first + second + second
    scratch += [pltpu.VMEM((SIZE[c], OWN, w), F32) for a, c, _, w, _ in STREAMS]
    dma = pltpu.SemaphoreType.DMA
    scratch += [dma((5,)), dma((6,)), dma((6,)), dma((8,)), dma((8,)), dma((5,)), dma((5,))]
    scratch += [dma((8 * n,)), dma((8 * n,)), dma((8 * n,)), dma((8 * n,))]
    hbm, smem = pl.BlockSpec(memory_space=pl.ANY), pl.BlockSpec(memory_space=pltpu.SMEM)
    result = pl.pallas_call(
        kernel,
        out_shape=jax.ShapeDtypeStruct((OWN, 3 * HID), F32),
        in_specs=[hbm] * 5 + [smem] * 3,
        out_specs=pl.BlockSpec(memory_space=pltpu.VMEM),
        scratch_shapes=scratch,
        compiler_params=pltpu.CompilerParams(
            collective_id=0, has_side_effects=True, vmem_limit_bytes=60 * 1024 * 1024
        ),
    )(tokens, grad_out, w_gate, w_lin, w_out_t, code, decode, stragglers)
    return result.reshape(OWN, 3, HID)


def solution(mesh):
    in_specs = (
        P("blk", "mp"),
        P("blk", "mp"),
        P(None, "mp"),
        P(None, "mp"),
        P(None, "mp"),
        P("blk", None),
        P("blk"),
        P(),
    )
    out_specs = P("blk", None, "mp")
    return jax.shard_map(shards, mesh=mesh, in_specs=in_specs, out_specs=out_specs, check_vma=False)
```

time: 238 us -> 68.8 us (0.29); the launches traced: 235 us -> 68.7 us
  blocking collectives: 185 us -> 0 us
  Pallas kernels: 0 us -> 66.4 us
  waiting for transfers between devices: 21.7 us -> 0 us
  starting transfers between devices: 6.46 us -> 0 us
  matrix products: 6.19 us -> 0 us
  other arithmetic: 6.13 us -> 0 us
  local copies, waits for them, and re-layouts: 5.88 us -> 1.65 us
  between operations: 4.07 us -> 0.66 us
    all_to_all x1 -> x0, blocking collectives: 185 us -> none  [sent_and_summed(): lax.all_to_all(in_blocks(shard, dim, peers), axis, 0, 0, tiled=True)]
    pallas_call x0 -> x1, Pallas kernels: none -> 66.4 us  [shards(): pl.pallas_call(kernel, out_shape=jax.ShapeDtypeStruct((OWN, 3 * HID), F32...]
    ppermute x4 -> x0, waiting for transfers between devices: 21.7 us -> none  [from_behind(): return lax.ppermute(block, axis, route)]
    dot_general x5 -> x0, matrix products: 6.19 us -> none  [the longest x1 2.35 us: local_grads(): linear = jnp.dot(inputs, w_lin, preferred_element_type=jnp.float32)]
    all_to_all x1 -> x0, starting transfers between devices: 4.29 us -> none  [sent_to_all(): return lax.all_to_all(copies, axis, split_axis=0, concat_axis=0, tiled=True)]
    slice x5 -> x0, local copies, waits for them, and re-layouts: 2.39 us -> none  [the longest x4 2.32 us: shards(): total_weight = total_weight + passed[slot]]
  transfers between devices with their start and end apart: 5 -> 0, of which waited for: 4 -> 0; matrix products, arithmetic and copies ran while one was open for 2% -> 0% of each run, Pallas kernels for 0% -> 0%
where the time goes in v1:
time: 68.8 us; the launch traced here: 68.7 us
  Pallas kernels  66.4 us (97%)
  local copies, waits for them, and re-layouts  1.65 us (2%)
    pallas_call x1, Pallas kernels, shards(): pl.pallas_call(kernel, out_shape=jax.ShapeDtypeStruct((OWN, 3 * HID), F32...  66.4 us
    reshape x1, local copies, waits for them, and re-layouts, shards(): return result.reshape(OWN, 3, HID)  1.65 us

profile of v1, /device:TPU:8, one launch (start us, length us, event | category | flops | bytes accessed | tf_op | source)
XLA Modules:
  0.0 68.7 jit_solution(1991459056571706929)
XLA Ops:
  0.7 66.4 %shard_map.82 = f32[32,1920]{1,0:T(8,128)} custom-call(bf16[128,512]{1,0:T(8,128)(2,1)} %tok.1, bf16[128,512]{1,0:T(8,128)(2,1)} %gout.1, bf16[2048,640]{1,0:T(8,128)(2,1)} %w_gate.1, bf16[2048,640]{1,0:T(8,128)(2,1)} %w_lin.1, bf16[2048,640]{1,0:T(8,128)(2,1)} %w_out.1, f32[1,5]{1,0:T(1,128)} %code.1, f32[1]{0:T(128)S(6)} %copy.14.decode, s32[4]{0:T(128)} %strag.1), custom_call_target="tpu_custom_call" | custom-call | tf_op jit(solution)/shard_map/pallas_call | solution.py:330
  67.0 1.7 %copy.13 = f32[4,3,8,640]{3,2,0,1:T(8,128)} copy(f32[4,3,8,640]{3,2,1,0:T(8,128)} %bitcast.4) | data formatting | bytes 491520 | tf_op jit(solution)/shard_map/reshape | solution.py:340

commit v2 on v1

v2 whole, which is shorter than its diff:
```python
import functools

import jax
import jax.numpy as jnp
from jax import lax
from jax.experimental import pallas as pl
from jax.experimental.pallas import tpu as pltpu
from jax.sharding import PartitionSpec as P

MESH = pl.DeviceIdType.MESH
BF16 = jnp.bfloat16
F32 = jnp.float32

NX, NY, NZ = 4, 4, 8
SIZE = {"y": NY, "z": NZ}
ROWS = 128
WIDTH = 512
HID = 640
OWN = 32
LANES = 128

STREAMS = (
    ("y", "z", 1408, 128, 1),
    ("y", "z", 640, 128, -1),
    ("y", "z", 896, 128, -1),
    ("y", "z", 1664, 128, -1),
    ("y", "z", 1152, 128, -1),
    ("z", "y", 1024, 128, 1),
    ("z", "y", 256, 256, -1),
    ("y", "z", 128, 128, 1),
    ("y", "z", 512, 128, 1),
    ("z", "y", 0, 128, 1),
    ("z", "y", 1792, 128, 1),
    ("z", "y", 1280, 128, 1),
    ("z", "y", 768, 128, -1),
    ("y", "z", 1536, 128, 1),
)
ORDER = (
    7, 7, 1, 1, 9, 9, 6, 6, 6, 7, 1, 0, 0, 9, 12, 12, 11, 11, 2, 2, 2, 13, 13, 9, 13, 7, 3, 1, 3, 5,
    5, 5, 12, 11, 0, 3, 8, 6, 8, 6, 8, 4, 4, 9, 4, 11, 10, 10, 12, 9, 2, 10, 0, 5, 5, 12, 11, 6, 1, 13,
    1, 1, 6, 11, 9, 10, 3, 7, 7, 7, 12, 9, 10, 5, 5, 12, 11, 8, 6, 1, 1, 4, 11, 10, 7, 7, 12, 2, 2, 0,
    0, 2, 9, 9, 10, 0, 9, 5, 3, 13, 13, 3, 13, 3, 11, 11, 11, 4, 8, 8, 4, 8, 6, 1, 10, 7, 6, 4, 0, 7,
    1, 9, 6, 12, 12, 12, 2, 2, 5, 5, 13, 5, 0, 11, 3, 3, 13, 8, 4, 8, 1, 6, 9, 10, 10, 10, 7, 12, 4, 2,
    0, 5, 2, 13, 0, 11, 3, 3, 13, 8, 4, 8, 1, 6, 10, 7, 12, 4, 2, 0, 5, 13, 3, 8, 4, 10, 2, 0, 13, 3,
    8, 4,
)
BLOCKS = ((0, 256), (256, 512), (512, 640))


def steps_of(n, sigma):
    half = n // 2
    steps = []
    for t in range(1, half + 1):
        step = [(sigma, half + 1 - t, t - 1, t - 2 if t > 1 else None)]
        if t < half:
            step.append((-sigma, half - t, half + t - 1, half + t - 2 if t > 1 else None))
        steps.append(step)
    return steps


def last_slots(n):
    return (n // 2 - 1, n - 2)


def gelu_parts(u):
    c = 0.7978845608028654
    t = jnp.tanh(c * (u + 0.044715 * (u * u * u)))
    half = 0.5 * (1.0 + t)
    act = u * half
    slope = half + 0.5 * u * (1.0 - t * t) * (c * (1.0 + 3.0 * 0.044715 * (u * u)))
    return act, slope


def kernel(
    tok, gout, w_gate, w_lin, w_out, code, decode, strag,
    out,
    code_s, decode_s, strag_s, stage,
    gath, wg, wl, wo, acc_g, acc_l, acc_h, dmat, xt, yt, prod, tab, ytab, *rest,
):
    n_streams = len(STREAMS)
    snd1, rcv1 = rest[:n_streams], rest[n_streams : 2 * n_streams]
    snd2, rcv2 = rest[2 * n_streams : 3 * n_streams], rest[3 * n_streams : 4 * n_streams]
    mid = rest[4 * n_streams : 5 * n_streams]
    (loc_sem, gs_sem, gr_sem, ds_sem, dr_sem, ws_sem, wr_sem, out_sem, s1, r1, s2, r2) = rest[5 * n_streams :]

    b = lax.axis_index("blk")
    m = lax.axis_index("mp")
    x_lo, yz = lax.div(b, NY * NZ), lax.rem(b, NY * NZ)
    y, z = lax.div(yz, NZ), lax.rem(yz, NZ)
    x_hi, core = lax.div(m, 2), lax.rem(m, 2)
    x = 2 * x_hi + x_lo
    me = {"y": y, "z": z}

    def device(px, py, pz, pc):
        return (lax.rem(px, 2) * (NY * NZ) + py * NZ + pz, lax.div(px, 2) * 2 + pc)

    def x_shift(d):
        return lax.rem(x + d + NX, NX)

    def ring_device(axis, d):
        q = lax.rem(me[axis] + d + SIZE[axis], SIZE[axis])
        return device(x, q, z, core) if axis == "y" else device(x, y, q, core)

    right, left = device(x_shift(1), y, z, core), device(x_shift(-1), y, z, core)
    sibling = device(x, y, z, 1 - core)
    pair = (lax.rem(b + NY * NZ, 2 * NY * NZ), m)

    barrier = pltpu.get_barrier_semaphore()
    partners = [right, left, sibling]
    partners += [ring_device(axis, d) for axis in ("y", "z") for d in (1, -1)]
    partners += [ring_device("z", -2)]
    for partner in partners:
        pl.semaphore_signal(barrier, inc=1, device_id=partner, device_id_type=MESH)

    smalls = [
        pltpu.make_async_copy(source, dest, loc_sem.at[5 + i])
        for i, (source, dest) in enumerate(((code, code_s), (decode, decode_s), (strag, strag_s)))
    ]
    for load in smalls:
        load.start()
    mine = pl.ds(pl.multiple_of(x_lo * ROWS, ROWS), ROWS)
    load_x = pltpu.make_async_copy(tok, gath.at[m, 0, mine, :], loc_sem.at[0])
    load_y = pltpu.make_async_copy(gout, gath.at[m, 1, mine, :], loc_sem.at[1])
    load_x.start()
    load_y.start()
    loads_w = [
        pltpu.make_async_copy(source, dest, loc_sem.at[2 + i])
        for i, (source, dest) in enumerate(((w_gate, wg), (w_lin, wl), (w_out, wo)))
    ]
    for load in loads_w:
        load.start()

    for load in smalls:
        load.wait()
    alive = (strag_s[0] != b) & (strag_s[1] != b) & (strag_s[2] != b) & (strag_s[3] != b)
    own_decode = jnp.where(alive, decode_s[0], 0.0)
    row_id = lax.broadcasted_iota(jnp.int32, (8, LANES), 0)
    coeffs = jnp.zeros((8, LANES), F32)
    for j in range(5):
        coeffs = jnp.where(row_id == j, own_decode * code_s[0, j], coeffs)
    tab[0, x_lo] = coeffs
    pl.semaphore_wait(barrier, len(partners))

    def remote(src, dst, ss, rs, to):
        return pltpu.make_async_remote_copy(
            src_ref=src, dst_ref=dst, send_sem=ss, recv_sem=rs, device_id=to, device_id_type=MESH
        )

    pending = []

    def go(src, dst, ss, rs, to):
        copy = remote(src, dst, ss, rs, to)
        copy.start()
        pending.append(copy)
        return copy

    def slot(px, pc, kind):
        rows = pl.ds(pl.multiple_of(lax.rem(px, 2) * ROWS, ROWS), ROWS)
        return gath.at[lax.div(px, 2) * 2 + pc, kind, rows, :]

    own_slot = [slot(x, core, k) for k in (0, 1)]
    swap = go(tab.at[0, x_lo], tab.at[0, x_lo], ws_sem.at[0], wr_sem.at[0], pair)
    load_x.wait()
    from_left = [None, None]
    from_right = [None, None]
    from_left[0] = go(own_slot[0], own_slot[0], gs_sem.at[0], gr_sem.at[0], right)
    load_y.wait()
    from_right[1] = go(own_slot[1], own_slot[1], gs_sem.at[3], gr_sem.at[3], left)
    from_left[1] = go(own_slot[1], own_slot[1], gs_sem.at[1], gr_sem.at[1], right)
    from_right[0] = go(own_slot[0], own_slot[0], gs_sem.at[2], gr_sem.at[2], left)
    sib = {}

    def to_sibling(rel, kind):
        src = slot(x_shift(rel), core, kind)
        idx = (rel % 4) * 2 + kind
        sib[rel, kind] = go(src, src, ds_sem.at[idx], dr_sem.at[idx], sibling)

    to_sibling(0, 0)
    to_sibling(0, 1)
    swap.wait_recv()
    near = [go(tab.at[0], tab.at[d], ws_sem.at[d], wr_sem.at[d], ring_device("z", d)) for d in (1, 2)]
    from_left[0].wait_recv()
    left_x = slot(x_shift(-1), core, 0)
    far_x = go(left_x, left_x, gs_sem.at[4], gr_sem.at[4], right)
    to_sibling(-1, 0)
    from_right[1].wait_recv()
    right_y = slot(x_shift(1), core, 1)
    far_y = go(right_y, right_y, gs_sem.at[5], gr_sem.at[5], left)
    to_sibling(1, 1)
    for copy in near:
        copy.wait_recv()
    farther = go(tab.at[pl.ds(1, 2)], tab.at[pl.ds(3, 2)], ws_sem.at[3], wr_sem.at[3], ring_device("z", 2))
    from_left[1].wait_recv()
    to_sibling(-1, 1)
    from_right[0].wait_recv()
    to_sibling(1, 0)
    farther.wait_recv()
    from_y = go(tab.at[pl.ds(1, 4)], ytab, ws_sem.at[4], wr_sem.at[4], ring_device("y", 1))
    for load in loads_w:
        load.wait()
    for rel in (0, -1, 1):
        for kind in (0, 1):
            sib[rel, kind].wait_recv()

    def forward(mm, first, lower=0, upper=HID):
        ks = pl.ds(pl.multiple_of(mm * WIDTH, WIDTH), WIDTH)
        cols = slice(lower, upper)
        for kind, w, acc in ((0, wg, acc_g), (0, wl, acc_l), (1, wo, acc_h)):
            part = jnp.dot(gath[mm, kind], w[ks, cols], preferred_element_type=F32)
            acc[:, cols] = part if first else acc[:, cols] + part

    forward(2 * x_hi, True)
    forward(2 * x_hi + 1, False)
    far_x.wait_recv()
    to_sibling(2, 0)
    far_y.wait_recv()
    to_sibling(2, 1)
    forward(2 * (1 - x_hi) + core, False)
    sib[2, 0].wait_recv()
    sib[2, 1].wait_recv()
    for i in range(2):
        xt[pl.ds(i * WIDTH, WIDTH), :] = gath[2 * x_lo + i, 0].T
        yt[pl.ds(i * WIDTH, WIDTH), :] = gath[2 * x_lo + i, 1].T
    from_y.wait_recv()
    weight = []
    for a in (0, 1):
        total = tab[0, a, 0:1, :]
        other = jnp.where(y == 0, 1 - a, a)
        for j in (1, 2, 3, 4):
            total = total + jnp.where(z >= j, tab[j, a, j : j + 1, :], ytab[j - 1, other, j : j + 1, :])
        weight.append(jnp.concatenate([total, total], axis=1))

    finished = set()

    def finish(block):
        lower, upper = BLOCKS[block]
        forward(2 * (1 - x_hi) + 1 - core, False, lower, upper)

        def elementwise(i, carry):
            rows = pl.ds(pl.multiple_of(i * 32, 32), 32)
            act, slope = gelu_parts(acc_g[rows, lower:upper])
            lin, dh = acc_l[rows, lower:upper], acc_h[rows, lower:upper]
            dmat[rows, lower:upper] = (dh * lin * slope).astype(BF16)
            dmat[rows, HID + lower : HID + upper] = (dh * act).astype(BF16)
            dmat[rows, 2 * HID + lower : 2 * HID + upper] = (act * lin).astype(BF16)
            return carry

        lax.fori_loop(0, 2 * ROWS // 32, elementwise, 0)

    def products(s):
        col, width = STREAMS[s][2:4]
        for block, (lower, upper) in enumerate(BLOCKS):
            if block not in finished and col % HID < upper and col % HID + width > lower:
                finished.add(block)
                finish(block)
        lhs = xt if col < 2 * HID else yt
        for yd in range(NY):
            rows = slice(yd * NZ * OWN, (yd + 1) * NZ * OWN)
            value = None
            for i in (0, 1):
                tokens = slice(i * ROWS, (i + 1) * ROWS)
                part = jnp.dot(lhs[rows, tokens], dmat[tokens, col : col + width], preferred_element_type=F32)
                part = weight[i][:, :width] * part
                value = part if value is None else value + part
            prod[yd, :, :, col : col + width] = value.reshape(NZ, OWN, width)

    def local1(s, d):
        axis, _, col, width, _ = STREAMS[s]
        cols = slice(col, col + width)
        return prod[:, d, :, cols] if axis == "z" else prod[d, :, :, cols]

    def run(s):
        axis1, axis2, col, width, sigma = STREAMS[s]
        yield
        products(s)
        for phase, axis, snd, rcv, ss, rs in ((1, axis1, snd1[s], rcv1[s], s1, r1), (2, axis2, snd2[s], rcv2[s], s2, r2)):
            n = SIZE[axis]
            local = functools.partial(local1, s) if phase == 1 else lambda d: mid[s][d]
            base = s * 8
            flying = {}
            for step in steps_of(n, sigma):
                for direction, distance, index, before in step:
                    yield
                    dest = lax.rem(me[axis] + direction * distance + n, n)
                    value = local(dest)
                    if before is not None:
                        flying[before].wait_recv()
                        value = value + rcv[before].astype(F32)
                    snd[index] = value.astype(BF16)
                    flying[index] = go(
                        snd.at[index], rcv.at[index], ss.at[base + index], rs.at[base + index],
                        ring_device(axis, direction),
                    )
            yield
            value = local(me[axis])
            for index in last_slots(n):
                flying[index].wait_recv()
                value = value + rcv[index].astype(F32)
            if phase == 1:
                mid[s][...] = value
            else:
                kind, cols = col // HID, pl.ds(col % HID, width)
                stage[kind, :, cols] = value
                written = pltpu.make_async_copy(stage.at[kind, :, cols], out.at[kind, :, cols], out_sem.at[s])
                written.start()
                writes.append(written)

    runs = [run(s) for s in range(n_streams)]
    writes = []
    for r in runs:
        next(r)
    for s in ORDER:
        next(runs[s], None)
    assert len(writes) == n_streams
    for written in writes:
        written.wait()
    for copy in pending:
        copy.wait_send()


def shards(tokens, grad_out, w_gate, w_lin, w_out_t, code, decode, stragglers):
    n = len(STREAMS)
    scratch = [
        pltpu.SMEM((1, 5), F32),
        pltpu.SMEM((1,), F32),
        pltpu.SMEM((4,), jnp.int32),
        pltpu.VMEM((3, OWN, HID), F32),
        pltpu.VMEM((4, 2, 2 * ROWS, WIDTH), BF16),
        pltpu.VMEM((4 * WIDTH, HID), BF16),
        pltpu.VMEM((4 * WIDTH, HID), BF16),
        pltpu.VMEM((4 * WIDTH, HID), BF16),
        pltpu.VMEM((2 * ROWS, HID), F32),
        pltpu.VMEM((2 * ROWS, HID), F32),
        pltpu.VMEM((2 * ROWS, HID), F32),
        pltpu.VMEM((2 * ROWS, 3 * HID), BF16),
        pltpu.VMEM((2 * WIDTH, 2 * ROWS), BF16),
        pltpu.VMEM((2 * WIDTH, 2 * ROWS), BF16),
        pltpu.VMEM((NY, NZ, OWN, 3 * HID), F32),
        pltpu.VMEM((5, 2, 8, LANES), F32),
        pltpu.VMEM((4, 2, 8, LANES), F32),
    ]
    first = [pltpu.VMEM((SIZE[a] - 1, SIZE[c], OWN, w), BF16) for a, c, _, w, _ in STREAMS]
    second = [pltpu.VMEM((SIZE[c] - 1, OWN, w), BF16) for a, c, _, w, _ in STREAMS]
    scratch += first + first + second + second
    scratch += [pltpu.VMEM((SIZE[c], OWN, w), F32) for a, c, _, w, _ in STREAMS]
    dma = pltpu.SemaphoreType.DMA
    scratch += [dma((8,)), dma((6,)), dma((6,)), dma((8,)), dma((8,)), dma((5,)), dma((5,)), dma((n,))]
    scratch += [dma((8 * n,)), dma((8 * n,)), dma((8 * n,)), dma((8 * n,))]
    hbm = pl.BlockSpec(memory_space=pl.ANY)
    result = pl.pallas_call(
        kernel,
        out_shape=jax.ShapeDtypeStruct((3, OWN, HID), F32),
        in_specs=[hbm] * 8,
        out_specs=hbm,
        scratch_shapes=scratch,
        compiler_params=pltpu.CompilerParams(
            collective_id=0, has_side_effects=True, vmem_limit_bytes=60 * 1024 * 1024
        ),
    )(tokens, grad_out, w_gate, w_lin, w_out_t, code, decode, stragglers)
    return jnp.swapaxes(result, 0, 1)


def solution(mesh):
    in_specs = (
        P("blk", "mp"),
        P("blk", "mp"),
        P(None, "mp"),
        P(None, "mp"),
        P(None, "mp"),
        P("blk", None),
        P("blk"),
        P(),
    )
    out_specs = P("blk", None, "mp")
    return jax.shard_map(shards, mesh=mesh, in_specs=in_specs, out_specs=out_specs, check_vma=False)
```

time: 68.8 us -> 63.1 us (0.917)
  Pallas kernels: 66.4 us -> 60.3 us
    pallas_call x1, Pallas kernels: 66.4 us -> 60.3 us  [shards(): pl.pallas_call(kernel, out_shape=jax.ShapeDtypeStruct((3, OWN, HID), F32)...]
    reshape x1 -> x0, local copies, waits for them, and re-layouts: 1.65 us -> none  [shards(): return result.reshape(OWN, 3, HID)]
    unnamed x0 -> x1, local copies, waits for them, and re-layouts: none -> 1.65 us
where the time goes in v2:
time: 63.1 us; the launch traced here: 62.6 us
  Pallas kernels  60.3 us (96%)
  local copies, waits for them, and re-layouts  1.65 us (3%)
  between operations  0.66 us (1%)
    pallas_call x1, Pallas kernels, shards(): pl.pallas_call(kernel, out_shape=jax.ShapeDtypeStruct((3, OWN, HID), F32)...  60.3 us
    unnamed x1, local copies, waits for them, and re-layouts  1.65 us

profile of v2, /device:TPU:8, one launch (start us, length us, event | category | flops | bytes accessed | tf_op | source)
XLA Modules:
  0.0 62.6 jit_solution(11791158725975537537)
XLA Ops:
  0.7 60.3 %shard_map.82 = f32[3,32,640]{2,1,0:T(8,128)} custom-call(bf16[128,512]{1,0:T(8,128)(2,1)} %tok.1, bf16[128,512]{1,0:T(8,128)(2,1)} %gout.1, bf16[2048,640]{1,0:T(8,128)(2,1)} %w_gate.1, bf16[2048,640]{1,0:T(8,128)(2,1)} %w_lin.1, bf16[2048,640]{1,0:T(8,128)(2,1)} %w_out.1, f32[1,5]{1,0:T(1,128)} %code.1, f32[1]{0:T(128)S(6)} %copy.10.decode, s32[4]{0:T(128)} %strag.1), custom_call_target="tpu_custom_call" | custom-call | tf_op jit(solution)/shard_map/pallas_call | solution.py:350
  61.0 1.7 %copy.11 = f32[32,3,640]{2,0,1:T(8,128)} copy(f32[32,3,640]{2,0,1:T(8,128)} %bitcast.1) | data formatting | bytes 491520

commit v3 on v2

--- a/solution.py
+++ b/solution.py
@@ -20,29 +20,23 @@
 LANES = 128
 
 STREAMS = (
-    ("y", "z", 1408, 128, 1),
-    ("y", "z", 640, 128, -1),
-    ("y", "z", 896, 128, -1),
-    ("y", "z", 1664, 128, -1),
-    ("y", "z", 1152, 128, -1),
-    ("z", "y", 1024, 128, 1),
-    ("z", "y", 256, 256, -1),
-    ("y", "z", 128, 128, 1),
-    ("y", "z", 512, 128, 1),
-    ("z", "y", 0, 128, 1),
-    ("z", "y", 1792, 128, 1),
-    ("z", "y", 1280, 128, 1),
-    ("z", "y", 768, 128, -1),
-    ("y", "z", 1536, 128, 1),
+    ("y", "z", 640, 256, -1, 0),
+    ("z", "y", 896, 256, 1, 0),
+    ("z", "y", 1792, 128, -1, 0),
+    ("y", "z", 0, 256, 1, 0),
+    ("y", "z", 1664, 128, -1, 0),
+    ("y", "z", 1152, 128, -1, 0),
+    ("z", "y", 256, 256, -1, 0),
+    ("y", "z", 1536, 128, 1, 0),
+    ("z", "y", 1280, 256, 1, 0),
+    ("y", "z", 512, 128, 1, 0),
 )
 ORDER = (
-    7, 7, 1, 1, 9, 9, 6, 6, 6, 7, 1, 0, 0, 9, 12, 12, 11, 11, 2, 2, 2, 13, 13, 9, 13, 7, 3, 1, 3, 5,
-    5, 5, 12, 11, 0, 3, 8, 6, 8, 6, 8, 4, 4, 9, 4, 11, 10, 10, 12, 9, 2, 10, 0, 5, 5, 12, 11, 6, 1, 13,
-    1, 1, 6, 11, 9, 10, 3, 7, 7, 7, 12, 9, 10, 5, 5, 12, 11, 8, 6, 1, 1, 4, 11, 10, 7, 7, 12, 2, 2, 0,
-    0, 2, 9, 9, 10, 0, 9, 5, 3, 13, 13, 3, 13, 3, 11, 11, 11, 4, 8, 8, 4, 8, 6, 1, 10, 7, 6, 4, 0, 7,
-    1, 9, 6, 12, 12, 12, 2, 2, 5, 5, 13, 5, 0, 11, 3, 3, 13, 8, 4, 8, 1, 6, 9, 10, 10, 10, 7, 12, 4, 2,
-    0, 5, 2, 13, 0, 11, 3, 3, 13, 8, 4, 8, 1, 6, 10, 7, 12, 4, 2, 0, 5, 13, 3, 8, 4, 10, 2, 0, 13, 3,
-    8, 4,
+    0, 0, 3, 3, 8, 8, 6, 6, 6, 1, 1, 0, 1, 8, 3, 4, 4, 7, 7, 4, 7, 9, 9, 9, 2, 2, 2, 5, 5, 5,
+    8, 0, 3, 6, 6, 1, 1, 8, 4, 2, 2, 8, 7, 6, 6, 1, 1, 9, 5, 8, 2, 2, 8, 6, 0, 0, 0, 3, 3, 3,
+    1, 4, 4, 4, 7, 7, 7, 5, 5, 5, 2, 9, 9, 9, 8, 8, 8, 3, 6, 6, 6, 0, 0, 3, 1, 4, 1, 1, 4, 7,
+    5, 7, 5, 9, 8, 2, 2, 2, 9, 3, 6, 0, 0, 3, 4, 1, 4, 7, 5, 5, 7, 9, 8, 2, 9, 3, 6, 0, 4, 1,
+    7, 5, 9, 2, 3, 0, 4, 7, 5, 9,
 )
 BLOCKS = ((0, 256), (256, 512), (512, 640))
 
@@ -51,15 +45,24 @@
     half = n // 2
     steps = []
     for t in range(1, half + 1):
-        step = [(sigma, half + 1 - t, t - 1, t - 2 if t > 1 else None)]
+        index = t - 1 if t < half else n - 3
+        steps.append((sigma, half + 1 - t, index, t - 2 if t > 1 else None))
         if t < half:
-            step.append((-sigma, half - t, half + t - 1, half + t - 2 if t > 1 else None))
-        steps.append(step)
+            index = half + t - 2 if t < half - 1 else n - 2
+            steps.append((-sigma, half - t, index, half + t - 3 if t > 1 else None))
     return steps
 
 
-def last_slots(n):
-    return (n // 2 - 1, n - 2)
+def sems_of(n, direct):
+    return 1 if direct else n - 2
+
+
+def counts():
+    first, total = [], 0
+    for a, c, _, _, _, direct in STREAMS:
+        first.append((total, total + sems_of(SIZE[a], 0)))
+        total = first[-1][1] + sems_of(SIZE[c], direct)
+    return first, total
 
 
 def gelu_parts(u):
@@ -81,7 +84,7 @@
     snd1, rcv1 = rest[:n_streams], rest[n_streams : 2 * n_streams]
     snd2, rcv2 = rest[2 * n_streams : 3 * n_streams], rest[3 * n_streams : 4 * n_streams]
     mid = rest[4 * n_streams : 5 * n_streams]
-    (loc_sem, gs_sem, gr_sem, ds_sem, dr_sem, ws_sem, wr_sem, out_sem, s1, r1, s2, r2) = rest[5 * n_streams :]
+    (loc_sem, gs_sem, gr_sem, ds_sem, dr_sem, ws_sem, wr_sem, out_sem, s_sem, r_sem) = rest[5 * n_streams :]
 
     b = lax.axis_index("blk")
     m = lax.axis_index("mp")
@@ -190,17 +193,12 @@
     for copy in near:
         copy.wait_recv()
     farther = go(tab.at[pl.ds(1, 2)], tab.at[pl.ds(3, 2)], ws_sem.at[3], wr_sem.at[3], ring_device("z", 2))
+    for load in loads_w:
+        load.wait()
     from_left[1].wait_recv()
     to_sibling(-1, 1)
     from_right[0].wait_recv()
     to_sibling(1, 0)
-    farther.wait_recv()
-    from_y = go(tab.at[pl.ds(1, 4)], ytab, ws_sem.at[4], wr_sem.at[4], ring_device("y", 1))
-    for load in loads_w:
-        load.wait()
-    for rel in (0, -1, 1):
-        for kind in (0, 1):
-            sib[rel, kind].wait_recv()
 
     def forward(mm, first, lower=0, upper=HID):
         ks = pl.ds(pl.multiple_of(mm * WIDTH, WIDTH), WIDTH)
@@ -209,18 +207,28 @@
             part = jnp.dot(gath[mm, kind], w[ks, cols], preferred_element_type=F32)
             acc[:, cols] = part if first else acc[:, cols] + part
 
-    forward(2 * x_hi, True)
-    forward(2 * x_hi + 1, False)
+    def transpose(a):
+        tokens = pl.ds(pl.multiple_of(a * ROWS, ROWS), ROWS)
+        for i in range(2):
+            xt[pl.ds(i * WIDTH, WIDTH), tokens] = gath[2 * x_lo + i, 0, tokens, :].T
+            yt[pl.ds(i * WIDTH, WIDTH), tokens] = gath[2 * x_lo + i, 1, tokens, :].T
+
+    forward(2 * x_hi + core, True)
+    for rel in (0, -1, 1):
+        for kind in (0, 1):
+            sib[rel, kind].wait_recv()
+    farther.wait_recv()
+    from_y = go(tab.at[pl.ds(1, 4)], ytab, ws_sem.at[4], wr_sem.at[4], ring_device("y", 1))
+    forward(2 * x_hi + 1 - core, False)
     far_x.wait_recv()
     to_sibling(2, 0)
     far_y.wait_recv()
     to_sibling(2, 1)
     forward(2 * (1 - x_hi) + core, False)
+    transpose(1 - x_lo)
     sib[2, 0].wait_recv()
     sib[2, 1].wait_recv()
-    for i in range(2):
-        xt[pl.ds(i * WIDTH, WIDTH), :] = gath[2 * x_lo + i, 0].T
-        yt[pl.ds(i * WIDTH, WIDTH), :] = gath[2 * x_lo + i, 1].T
+    transpose(x_lo)
     from_y.wait_recv()
     weight = []
     for a in (0, 1):
@@ -265,38 +273,46 @@
             prod[yd, :, :, col : col + width] = value.reshape(NZ, OWN, width)
 
     def local1(s, d):
-        axis, _, col, width, _ = STREAMS[s]
+        axis, _, col, width = STREAMS[s][:4]
         cols = slice(col, col + width)
         return prod[:, d, :, cols] if axis == "z" else prod[d, :, :, cols]
 
     def run(s):
-        axis1, axis2, col, width, sigma = STREAMS[s]
+        axis1, axis2, col, width, sigma, direct2 = STREAMS[s]
         yield
         products(s)
-        for phase, axis, snd, rcv, ss, rs in ((1, axis1, snd1[s], rcv1[s], s1, r1), (2, axis2, snd2[s], rcv2[s], s2, r2)):
+        for phase, axis, snd, rcv in ((0, axis1, snd1[s], rcv1[s]), (1, axis2, snd2[s], rcv2[s])):
             n = SIZE[axis]
-            local = functools.partial(local1, s) if phase == 1 else lambda d: mid[s][d]
-            base = s * 8
-            flying = {}
-            for step in steps_of(n, sigma):
-                for direction, distance, index, before in step:
+            local = functools.partial(local1, s) if phase == 0 else lambda d: mid[s][d]
+            ss, base = s_sem.at[2 * s + phase], first_sem[s][phase]
+            sent.append((snd, ss))
+            if phase and direct2:
+                for k in range(n - 1, 0, -1):
                     yield
-                    dest = lax.rem(me[axis] + direction * distance + n, n)
-                    value = local(dest)
+                    snd[k - 1] = local(lax.rem(me[axis] + k, n)).astype(BF16)
+                    to = ring_device(axis, k if 2 * k <= n else k - n)
+                    remote(snd.at[k - 1], rcv.at[k - 1], ss, r_sem.at[base], to).start()
+                yield
+                remote(snd, rcv, ss, r_sem.at[base], sibling).wait_recv()
+                arrived = range(n - 1)
+            else:
+                for direction, distance, index, before in steps_of(n, sigma):
+                    yield
+                    value = local(lax.rem(me[axis] + direction * distance + n, n))
+                    to = ring_device(axis, direction)
                     if before is not None:
-                        flying[before].wait_recv()
+                        remote(snd.at[before], rcv.at[before], ss, r_sem.at[base + before], to).wait_recv()
                         value = value + rcv[before].astype(F32)
                     snd[index] = value.astype(BF16)
-                    flying[index] = go(
-                        snd.at[index], rcv.at[index], ss.at[base + index], rs.at[base + index],
-                        ring_device(axis, direction),
-                    )
-            yield
+                    remote(snd.at[index], rcv.at[index], ss, r_sem.at[base + min(index, n - 3)], to).start()
+                yield
+                last = pl.ds(n - 3, 2)
+                remote(snd.at[last], rcv.at[last], ss, r_sem.at[base + n - 3], sibling).wait_recv()
+                arrived = (n - 3, n - 2)
             value = local(me[axis])
-            for index in last_slots(n):
-                flying[index].wait_recv()
+            for index in arrived:
                 value = value + rcv[index].astype(F32)
-            if phase == 1:
+            if phase == 0:
                 mid[s][...] = value
             else:
                 kind, cols = col // HID, pl.ds(col % HID, width)
@@ -305,6 +321,8 @@
                 written.start()
                 writes.append(written)
 
+    first_sem, _ = counts()
+    sent = []
     runs = [run(s) for s in range(n_streams)]
     writes = []
     for r in runs:
@@ -314,6 +332,8 @@
     assert len(writes) == n_streams
     for written in writes:
         written.wait()
+    for snd, ss in sent:
+        remote(snd, snd, ss, r_sem.at[0], sibling).wait_send()
     for copy in pending:
         copy.wait_send()
 
@@ -339,13 +359,13 @@
         pltpu.VMEM((5, 2, 8, LANES), F32),
         pltpu.VMEM((4, 2, 8, LANES), F32),
     ]
-    first = [pltpu.VMEM((SIZE[a] - 1, SIZE[c], OWN, w), BF16) for a, c, _, w, _ in STREAMS]
-    second = [pltpu.VMEM((SIZE[c] - 1, OWN, w), BF16) for a, c, _, w, _ in STREAMS]
+    first = [pltpu.VMEM((SIZE[a] - 1, SIZE[c], OWN, w), BF16) for a, c, _, w, _, _ in STREAMS]
+    second = [pltpu.VMEM((SIZE[c] - 1, OWN, w), BF16) for a, c, _, w, _, _ in STREAMS]
     scratch += first + first + second + second
-    scratch += [pltpu.VMEM((SIZE[c], OWN, w), F32) for a, c, _, w, _ in STREAMS]
+    scratch += [pltpu.VMEM((SIZE[c], OWN, w), F32) for a, c, _, w, _, _ in STREAMS]
     dma = pltpu.SemaphoreType.DMA
     scratch += [dma((8,)), dma((6,)), dma((6,)), dma((8,)), dma((8,)), dma((5,)), dma((5,)), dma((n,))]
-    scratch += [dma((8 * n,)), dma((8 * n,)), dma((8 * n,)), dma((8 * n,))]
+    scratch += [dma((2 * n,)), dma((counts()[1],))]
     hbm = pl.BlockSpec(memory_space=pl.ANY)
     result = pl.pallas_call(
         kernel,

time: 63.1 us -> 59.2 us (0.938)
  Pallas kernels: 60.3 us -> 56 us
    pallas_call x1, Pallas kernels: 60.3 us -> 56 us  [shards(): pl.pallas_call(kernel, out_shape=jax.ShapeDtypeStruct((3, OWN, HID), F32)...]
where the time goes in v3:
time: 59.2 us; the launch traced here: 58.3 us
  Pallas kernels  56 us (95%)
  local copies, waits for them, and re-layouts  1.65 us (3%)
  between operations  0.66 us (1%)
    pallas_call x1, Pallas kernels, shards(): pl.pallas_call(kernel, out_shape=jax.ShapeDtypeStruct((3, OWN, HID), F32)...  56 us
    unnamed x1, local copies, waits for them, and re-layouts  1.65 us

profile of v3, /device:TPU:8, one launch (start us, length us, event | category | flops | bytes accessed | tf_op | source)
XLA Modules:
  0.0 58.3 jit_solution(17899697540641011605)
XLA Ops:
  0.7 56.0 %shard_map.82 = f32[3,32,640]{2,1,0:T(8,128)} custom-call(bf16[128,512]{1,0:T(8,128)(2,1)} %tok.1, bf16[128,512]{1,0:T(8,128)(2,1)} %gout.1, bf16[2048,640]{1,0:T(8,128)(2,1)} %w_gate.1, bf16[2048,640]{1,0:T(8,128)(2,1)} %w_lin.1, bf16[2048,640]{1,0:T(8,128)(2,1)} %w_out.1, f32[1,5]{1,0:T(1,128)} %code.1, f32[1]{0:T(128)S(6)} %copy.10.decode, s32[4]{0:T(128)} %strag.1), custom_call_target="tpu_custom_call" | custom-call | tf_op jit(solution)/shard_map/pallas_call | solution.py:370
  56.6 1.7 %copy.11 = f32[32,3,640]{2,0,1:T(8,128)} copy(f32[32,3,640]{2,0,1:T(8,128)} %bitcast.1) | data formatting | bytes 491520

commit v4 on v3

--- a/solution.py
+++ b/solution.py
@@ -20,48 +20,57 @@
 LANES = 128
 
 STREAMS = (
-    ("y", "z", 640, 256, -1, 0),
-    ("z", "y", 896, 256, 1, 0),
+    ("y", "z", 1280, 128, 1, 0),
+    ("z", "y", 1152, 128, 1, 0),
+    ("y", "z", 512, 128, 1, 0),
+    ("y", "z", 256, 128, 1, 1),
+    ("y", "z", 1536, 256, 1, 1),
+    ("y", "z", 0, 256, -1, 0),
+    ("y", "z", 384, 128, 1, 1),
+    ("z", "y", 640, 256, 1, 0),
     ("z", "y", 1792, 128, -1, 0),
-    ("y", "z", 0, 256, 1, 0),
-    ("y", "z", 1664, 128, -1, 0),
-    ("y", "z", 1152, 128, -1, 0),
-    ("z", "y", 256, 256, -1, 0),
-    ("y", "z", 1536, 128, 1, 0),
-    ("z", "y", 1280, 256, 1, 0),
-    ("y", "z", 512, 128, 1, 0),
+    ("z", "y", 896, 256, -1, 0),
+    ("z", "y", 1408, 128, -1, 0),
 )
 ORDER = (
-    0, 0, 3, 3, 8, 8, 6, 6, 6, 1, 1, 0, 1, 8, 3, 4, 4, 7, 7, 4, 7, 9, 9, 9, 2, 2, 2, 5, 5, 5,
-    8, 0, 3, 6, 6, 1, 1, 8, 4, 2, 2, 8, 7, 6, 6, 1, 1, 9, 5, 8, 2, 2, 8, 6, 0, 0, 0, 3, 3, 3,
-    1, 4, 4, 4, 7, 7, 7, 5, 5, 5, 2, 9, 9, 9, 8, 8, 8, 3, 6, 6, 6, 0, 0, 3, 1, 4, 1, 1, 4, 7,
-    5, 7, 5, 9, 8, 2, 2, 2, 9, 3, 6, 0, 0, 3, 4, 1, 4, 7, 5, 5, 7, 9, 8, 2, 9, 3, 6, 0, 4, 1,
-    7, 5, 9, 2, 3, 0, 4, 7, 5, 9,
+    2, 2, 2, 1, 1, 1, 8, 8, 8, 0, 0, 0, 10, 10, 10, 7, 7, 7, 5, 5, 5, 9, 1, 1, 9, 9, 6, 6, 6, 4,
+    2, 8, 8, 4, 4, 3, 3, 3, 10, 10, 0, 7, 7, 1, 1, 5, 9, 9, 8, 8, 6, 10, 10, 2, 2, 2, 7, 7, 1, 9,
+    9, 4, 8, 10, 3, 2, 2, 5, 5, 0, 0, 0, 5, 7, 1, 1, 1, 6, 6, 6, 6, 6, 9, 8, 8, 8, 2, 0, 10, 10,
+    10, 2, 5, 5, 0, 4, 4, 4, 4, 4, 7, 7, 7, 8, 3, 3, 3, 3, 3, 1, 2, 6, 10, 0, 6, 6, 9, 9, 9, 5,
+    5, 0, 7, 8, 4, 1, 10, 4, 4, 2, 3, 9, 3, 3, 0, 5, 6, 7, 4, 9, 0, 3, 5,
 )
 BLOCKS = ((0, 256), (256, 512), (512, 640))
 
 
-def steps_of(n, sigma):
+def schedule(n, sigma, two_stage):
     half = n // 2
-    steps = []
+    if two_stage:
+        messages = [
+            (sigma, 2, 4, 0, None),
+            (sigma, 2, 3, 1, None),
+            (-sigma, 2, 3, 2, None),
+            (-sigma, 2, 2, 3, None),
+            (sigma, 2, 2, 4, 0),
+            (sigma, 1, 1, 5, 1),
+            (-sigma, 1, 1, 6, 2),
+        ]
+        return messages, 4
+    messages = []
     for t in range(1, half + 1):
         index = t - 1 if t < half else n - 3
-        steps.append((sigma, half + 1 - t, index, t - 2 if t > 1 else None))
+        messages.append((sigma, 1, half + 1 - t, index, t - 2 if t > 1 else None))
         if t < half:
             index = half + t - 2 if t < half - 1 else n - 2
-            steps.append((-sigma, half - t, index, half + t - 3 if t > 1 else None))
-    return steps
-
-
-def sems_of(n, direct):
-    return 1 if direct else n - 2
+            messages.append((-sigma, 1, half - t, index, half + t - 3 if t > 1 else None))
+    return messages, 2
 
 
 def counts():
     first, total = [], 0
-    for a, c, _, _, _, direct in STREAMS:
-        first.append((total, total + sems_of(SIZE[a], 0)))
-        total = first[-1][1] + sems_of(SIZE[c], direct)
+    for a, c, _, _, sigma, two_stage in STREAMS:
+        middle = total + SIZE[a] - schedule(SIZE[a], sigma, 0)[1]
+        first.append((total, middle))
+        total = middle + SIZE[c] - schedule(SIZE[c], sigma, two_stage)[1]
     return first, total
 
 
@@ -111,7 +120,7 @@
     barrier = pltpu.get_barrier_semaphore()
     partners = [right, left, sibling]
     partners += [ring_device(axis, d) for axis in ("y", "z") for d in (1, -1)]
-    partners += [ring_device("z", -2)]
+    partners += [ring_device("z", d) for d in (2, -2)]
     for partner in partners:
         pl.semaphore_signal(barrier, inc=1, device_id=partner, device_id_type=MESH)
 
@@ -278,7 +287,7 @@
         return prod[:, d, :, cols] if axis == "z" else prod[d, :, :, cols]
 
     def run(s):
-        axis1, axis2, col, width, sigma, direct2 = STREAMS[s]
+        axis1, axis2, col, width, sigma, two_stage = STREAMS[s]
         yield
         products(s)
         for phase, axis, snd, rcv in ((0, axis1, snd1[s], rcv1[s]), (1, axis2, snd2[s], rcv2[s])):
@@ -286,29 +295,21 @@
             local = functools.partial(local1, s) if phase == 0 else lambda d: mid[s][d]
             ss, base = s_sem.at[2 * s + phase], first_sem[s][phase]
             sent.append((snd, ss))
-            if phase and direct2:
-                for k in range(n - 1, 0, -1):
-                    yield
-                    snd[k - 1] = local(lax.rem(me[axis] + k, n)).astype(BF16)
-                    to = ring_device(axis, k if 2 * k <= n else k - n)
-                    remote(snd.at[k - 1], rcv.at[k - 1], ss, r_sem.at[base], to).start()
+            messages, finals = schedule(n, sigma, phase and two_stage)
+            middle = n - 1 - finals
+            for direction, hops, distance, index, before in messages:
                 yield
-                remote(snd, rcv, ss, r_sem.at[base], sibling).wait_recv()
-                arrived = range(n - 1)
-            else:
-                for direction, distance, index, before in steps_of(n, sigma):
-                    yield
-                    value = local(lax.rem(me[axis] + direction * distance + n, n))
-                    to = ring_device(axis, direction)
-                    if before is not None:
-                        remote(snd.at[before], rcv.at[before], ss, r_sem.at[base + before], to).wait_recv()
-                        value = value + rcv[before].astype(F32)
-                    snd[index] = value.astype(BF16)
-                    remote(snd.at[index], rcv.at[index], ss, r_sem.at[base + min(index, n - 3)], to).start()
-                yield
-                last = pl.ds(n - 3, 2)
-                remote(snd.at[last], rcv.at[last], ss, r_sem.at[base + n - 3], sibling).wait_recv()
-                arrived = (n - 3, n - 2)
+                value = local(lax.rem(me[axis] + direction * distance + n, n))
+                to = ring_device(axis, direction * hops)
+                if before is not None:
+                    remote(snd.at[before], rcv.at[before], ss, r_sem.at[base + before], to).wait_recv()
+                    value = value + rcv[before].astype(F32)
+                snd[index] = value.astype(BF16)
+                remote(snd.at[index], rcv.at[index], ss, r_sem.at[base + min(index, middle)], to).start()
+            yield
+            last = pl.ds(middle, finals)
+            remote(snd.at[last], rcv.at[last], ss, r_sem.at[base + middle], sibling).wait_recv()
+            arrived = range(middle, n - 1)
             value = local(me[axis])
             for index in arrived:
                 value = value + rcv[index].astype(F32)
@@ -316,22 +317,15 @@
                 mid[s][...] = value
             else:
                 kind, cols = col // HID, pl.ds(col % HID, width)
-                stage[kind, :, cols] = value
-                written = pltpu.make_async_copy(stage.at[kind, :, cols], out.at[kind, :, cols], out_sem.at[s])
-                written.start()
-                writes.append(written)
+                out[kind, :, cols] = value
 
     first_sem, _ = counts()
     sent = []
     runs = [run(s) for s in range(n_streams)]
-    writes = []
     for r in runs:
         next(r)
     for s in ORDER:
         next(runs[s], None)
-    assert len(writes) == n_streams
-    for written in writes:
-        written.wait()
     for snd, ss in sent:
         remote(snd, snd, ss, r_sem.at[0], sibling).wait_send()
     for copy in pending:
@@ -369,9 +363,9 @@
     hbm = pl.BlockSpec(memory_space=pl.ANY)
     result = pl.pallas_call(
         kernel,
-        out_shape=jax.ShapeDtypeStruct((3, OWN, HID), F32),
+        out_shape=pltpu.VMEM((3, OWN, HID), F32),
         in_specs=[hbm] * 8,
-        out_specs=hbm,
+        out_specs=pl.BlockSpec(memory_space=pltpu.VMEM),
         scratch_shapes=scratch,
         compiler_params=pltpu.CompilerParams(
             collective_id=0, has_side_effects=True, vmem_limit_bytes=60 * 1024 * 1024

time: 59.2 us -> 55.2 us (0.932); the launches traced: 58.3 us -> 54.9 us
  Pallas kernels: 56 us -> 53.6 us
  local copies, waits for them, and re-layouts: 1.65 us -> 0.7 us
    pallas_call x1, Pallas kernels: 56 us -> 53.6 us  [shards(): pl.pallas_call(kernel, out_shape=pltpu.VMEM((3, OWN, HID), F32), in_specs...]
    unnamed x1, local copies, waits for them, and re-layouts: 1.65 us -> 0.7 us
where the time goes in v4:
time: 55.2 us; the launch traced here: 54.9 us
  Pallas kernels  53.6 us (97%)
  local copies, waits for them, and re-layouts  0.7 us (1%)
  between operations  0.66 us (1%)
    pallas_call x1, Pallas kernels, shards(): pl.pallas_call(kernel, out_shape=pltpu.VMEM((3, OWN, HID), F32), in_specs...  53.6 us

profile of v4, /device:TPU:8, one launch (start us, length us, event | category | flops | bytes accessed | tf_op | source)
XLA Modules:
  0.0 54.9 jit_solution(13419516713926384937)
XLA Ops:
  0.7 53.6 %shard_map.82 = f32[3,32,640]{2,1,0:T(8,128)S(1)} custom-call(bf16[128,512]{1,0:T(8,128)(2,1)} %tok.1, bf16[128,512]{1,0:T(8,128)(2,1)} %gout.1, bf16[2048,640]{1,0:T(8,128)(2,1)} %w_gate.1, bf16[2048,640]{1,0:T(8,128)(2,1)} %w_lin.1, bf16[2048,640]{1,0:T(8,128)(2,1)} %w_out.1, f32[1,5]{1,0:T(1,128)} %code.1, f32[1]{0:T(128)S(6)} %copy.11.decode, s32[4]{0:T(128)} %strag.1), custom_call_target="tpu_custom_call" | custom-call | tf_op jit(solution)/shard_map/pallas_call | solution.py:364
  54.2 0.7 %copy.10 = f32[32,3,640]{2,0,1:T(8,128)} copy(f32[32,3,640]{2,0,1:T(8,128)S(1)} %bitcast.1) | data formatting | bytes 491520

commit v5 on v4

--- a/solution.py
+++ b/solution.py
@@ -20,30 +20,31 @@
 LANES = 128
 
 STREAMS = (
-    ("y", "z", 1280, 128, 1, 0),
-    ("z", "y", 1152, 128, 1, 0),
-    ("y", "z", 512, 128, 1, 0),
-    ("y", "z", 256, 128, 1, 1),
-    ("y", "z", 1536, 256, 1, 1),
-    ("y", "z", 0, 256, -1, 0),
-    ("y", "z", 384, 128, 1, 1),
-    ("z", "y", 640, 256, 1, 0),
-    ("z", "y", 1792, 128, -1, 0),
-    ("z", "y", 896, 256, -1, 0),
-    ("z", "y", 1408, 128, -1, 0),
+    ("y", "z", 1280, 128, -1, 1),
+    ("y", "z", 0, 128, 1, 1),
+    ("y", "z", 1408, 128, 1, 0),
+    ("z", "y", 1536, 128, -1, 0),
+    ("z", "y", 1664, 256, -1, 0),
+    ("y", "z", 640, 128, -1, 1),
+    ("z", "y", 768, 256, 1, 0),
+    ("y", "z", 384, 256, -1, 1),
+    ("y", "z", 1024, 256, 1, 1),
+    ("z", "y", 128, 256, 1, 0),
 )
 ORDER = (
-    2, 2, 2, 1, 1, 1, 8, 8, 8, 0, 0, 0, 10, 10, 10, 7, 7, 7, 5, 5, 5, 9, 1, 1, 9, 9, 6, 6, 6, 4,
-    2, 8, 8, 4, 4, 3, 3, 3, 10, 10, 0, 7, 7, 1, 1, 5, 9, 9, 8, 8, 6, 10, 10, 2, 2, 2, 7, 7, 1, 9,
-    9, 4, 8, 10, 3, 2, 2, 5, 5, 0, 0, 0, 5, 7, 1, 1, 1, 6, 6, 6, 6, 6, 9, 8, 8, 8, 2, 0, 10, 10,
-    10, 2, 5, 5, 0, 4, 4, 4, 4, 4, 7, 7, 7, 8, 3, 3, 3, 3, 3, 1, 2, 6, 10, 0, 6, 6, 9, 9, 9, 5,
-    5, 0, 7, 8, 4, 1, 10, 4, 4, 2, 3, 9, 3, 3, 0, 5, 6, 7, 4, 9, 0, 3, 5,
+    2, 2, 2, 3, 3, 3, 9, 9, 9, 8, 8, 8, 4, 4, 4, 6, 6, 6, 0, 0, 0, 5, 5, 5, 7, 3, 3, 7, 1, 2,
+    1, 7, 1, 9, 9, 4, 4, 8, 6, 6, 3, 3, 0, 9, 9, 5, 4, 4, 2, 2, 2, 6, 6, 7, 1, 3, 9, 0, 0, 0,
+    0, 0, 4, 2, 2, 5, 5, 5, 5, 5, 6, 8, 8, 8, 8, 8, 3, 3, 3, 9, 9, 9, 1, 1, 7, 7, 7, 7, 0, 1,
+    1, 7, 1, 0, 2, 0, 4, 4, 4, 2, 3, 5, 9, 6, 6, 6, 5, 5, 8, 4, 8, 3, 8, 7, 1, 7, 9, 7, 6, 1,
+    1, 2, 0, 4, 5, 8, 6, 7, 1, 2,
 )
-BLOCKS = ((0, 256), (256, 512), (512, 640))
+BLOCKS = ((0, 128), (128, 384), (384, 640))
 
 
 def schedule(n, sigma, two_stage):
     half = n // 2
+    if two_stage and n == 4:
+        return [(sigma, 2, 2, 0, None), (1, 1, 1, 1, None), (-1, 1, 1, 2, None)], 3
     if two_stage:
         messages = [
             (sigma, 2, 4, 0, None),
@@ -86,14 +87,14 @@
 def kernel(
     tok, gout, w_gate, w_lin, w_out, code, decode, strag,
     out,
-    code_s, decode_s, strag_s, stage,
-    gath, wg, wl, wo, acc_g, acc_l, acc_h, dmat, xt, yt, prod, tab, ytab, *rest,
+    code_s, decode_s, strag_s,
+    gath, wts, acc_g, acc_l, acc_h, dmat, xt, yt, prod, tab, ytab, *rest,
 ):
     n_streams = len(STREAMS)
     snd1, rcv1 = rest[:n_streams], rest[n_streams : 2 * n_streams]
     snd2, rcv2 = rest[2 * n_streams : 3 * n_streams], rest[3 * n_streams : 4 * n_streams]
     mid = rest[4 * n_streams : 5 * n_streams]
-    (loc_sem, gs_sem, gr_sem, ds_sem, dr_sem, ws_sem, wr_sem, out_sem, s_sem, r_sem) = rest[5 * n_streams :]
+    (loc_sem, gs_sem, gr_sem, dr_sem, ws_sem, wr_sem, s_sem, r_sem) = rest[5 * n_streams :]
 
     b = lax.axis_index("blk")
     m = lax.axis_index("mp")
@@ -117,30 +118,25 @@
     sibling = device(x, y, z, 1 - core)
     pair = (lax.rem(b + NY * NZ, 2 * NY * NZ), m)
 
+    mine = pl.ds(pl.multiple_of(x_lo * ROWS, ROWS), ROWS)
+    load_x = pltpu.make_async_copy(tok, gath.at[m, 0, mine, :], loc_sem.at[0])
+    load_y = pltpu.make_async_copy(gout, gath.at[m, 1, mine, :], loc_sem.at[1])
+    smalls = [
+        pltpu.make_async_copy(source, dest, loc_sem.at[3 + i])
+        for i, (source, dest) in enumerate(((code, code_s), (decode, decode_s), (strag, strag_s)))
+    ]
+    for load in (load_x, load_y, *smalls):
+        load.start()
+
     barrier = pltpu.get_barrier_semaphore()
     partners = [right, left, sibling]
     partners += [ring_device(axis, d) for axis in ("y", "z") for d in (1, -1)]
-    partners += [ring_device("z", d) for d in (2, -2)]
+    partners += [ring_device(axis, d) for axis in ("z",) for d in (2, -2)]
     for partner in partners:
         pl.semaphore_signal(barrier, inc=1, device_id=partner, device_id_type=MESH)
 
-    smalls = [
-        pltpu.make_async_copy(source, dest, loc_sem.at[5 + i])
-        for i, (source, dest) in enumerate(((code, code_s), (decode, decode_s), (strag, strag_s)))
-    ]
-    for load in smalls:
-        load.start()
-    mine = pl.ds(pl.multiple_of(x_lo * ROWS, ROWS), ROWS)
-    load_x = pltpu.make_async_copy(tok, gath.at[m, 0, mine, :], loc_sem.at[0])
-    load_y = pltpu.make_async_copy(gout, gath.at[m, 1, mine, :], loc_sem.at[1])
-    load_x.start()
-    load_y.start()
-    loads_w = [
-        pltpu.make_async_copy(source, dest, loc_sem.at[2 + i])
-        for i, (source, dest) in enumerate(((w_gate, wg), (w_lin, wl), (w_out, wo)))
-    ]
-    for load in loads_w:
-        load.start()
+    for i, source in enumerate((w_gate, w_lin, w_out)):
+        pltpu.make_async_copy(source, wts.at[i], loc_sem.at[2]).start()
 
     for load in smalls:
         load.wait()
@@ -160,11 +156,13 @@
 
     pending = []
 
-    def go(src, dst, ss, rs, to):
+    def go(src, dst, ss, rs, to, kept=pending):
         copy = remote(src, dst, ss, rs, to)
         copy.start()
-        pending.append(copy)
+        kept.append(copy)
         return copy
+
+    shared = []
 
     def slot(px, pc, kind):
         rows = pl.ds(pl.multiple_of(lax.rem(px, 2) * ROWS, ROWS), ROWS)
@@ -175,17 +173,17 @@
     load_x.wait()
     from_left = [None, None]
     from_right = [None, None]
-    from_left[0] = go(own_slot[0], own_slot[0], gs_sem.at[0], gr_sem.at[0], right)
+    from_left[0] = go(own_slot[0], own_slot[0], gs_sem.at[0], gr_sem.at[0], right, shared)
     load_y.wait()
-    from_right[1] = go(own_slot[1], own_slot[1], gs_sem.at[3], gr_sem.at[3], left)
-    from_left[1] = go(own_slot[1], own_slot[1], gs_sem.at[1], gr_sem.at[1], right)
-    from_right[0] = go(own_slot[0], own_slot[0], gs_sem.at[2], gr_sem.at[2], left)
+    from_right[1] = go(own_slot[1], own_slot[1], gs_sem.at[0], gr_sem.at[3], left, shared)
+    from_left[1] = go(own_slot[1], own_slot[1], gs_sem.at[0], gr_sem.at[1], right, shared)
+    from_right[0] = go(own_slot[0], own_slot[0], gs_sem.at[0], gr_sem.at[2], left, shared)
     sib = {}
 
     def to_sibling(rel, kind):
         src = slot(x_shift(rel), core, kind)
         idx = (rel % 4) * 2 + kind
-        sib[rel, kind] = go(src, src, ds_sem.at[idx], dr_sem.at[idx], sibling)
+        sib[rel, kind] = go(src, src, gs_sem.at[0], dr_sem.at[idx], sibling, shared)
 
     to_sibling(0, 0)
     to_sibling(0, 1)
@@ -193,17 +191,16 @@
     near = [go(tab.at[0], tab.at[d], ws_sem.at[d], wr_sem.at[d], ring_device("z", d)) for d in (1, 2)]
     from_left[0].wait_recv()
     left_x = slot(x_shift(-1), core, 0)
-    far_x = go(left_x, left_x, gs_sem.at[4], gr_sem.at[4], right)
+    far_x = go(left_x, left_x, gs_sem.at[1], gr_sem.at[4], right, shared)
     to_sibling(-1, 0)
     from_right[1].wait_recv()
     right_y = slot(x_shift(1), core, 1)
-    far_y = go(right_y, right_y, gs_sem.at[5], gr_sem.at[5], left)
+    far_y = go(right_y, right_y, gs_sem.at[1], gr_sem.at[5], left, shared)
     to_sibling(1, 1)
     for copy in near:
         copy.wait_recv()
     farther = go(tab.at[pl.ds(1, 2)], tab.at[pl.ds(3, 2)], ws_sem.at[3], wr_sem.at[3], ring_device("z", 2))
-    for load in loads_w:
-        load.wait()
+    pltpu.make_async_copy(wts, wts, loc_sem.at[2]).wait()
     from_left[1].wait_recv()
     to_sibling(-1, 1)
     from_right[0].wait_recv()
@@ -212,8 +209,8 @@
     def forward(mm, first, lower=0, upper=HID):
         ks = pl.ds(pl.multiple_of(mm * WIDTH, WIDTH), WIDTH)
         cols = slice(lower, upper)
-        for kind, w, acc in ((0, wg, acc_g), (0, wl, acc_l), (1, wo, acc_h)):
-            part = jnp.dot(gath[mm, kind], w[ks, cols], preferred_element_type=F32)
+        for i, (kind, acc) in enumerate(((0, acc_g), (0, acc_l), (1, acc_h))):
+            part = jnp.dot(gath[mm, kind], wts[i, ks, cols], preferred_element_type=F32)
             acc[:, cols] = part if first else acc[:, cols] + part
 
     def transpose(a):
@@ -330,6 +327,9 @@
         remote(snd, snd, ss, r_sem.at[0], sibling).wait_send()
     for copy in pending:
         copy.wait_send()
+    assert len(shared) == 14
+    remote(gath.at[0:3], gath.at[0:3], gs_sem.at[0], gr_sem.at[0], sibling).wait_send()
+    remote(gath.at[3, 0], gath.at[3, 0], gs_sem.at[1], gr_sem.at[0], sibling).wait_send()
 
 
 def shards(tokens, grad_out, w_gate, w_lin, w_out_t, code, decode, stragglers):
@@ -338,11 +338,8 @@
         pltpu.SMEM((1, 5), F32),
         pltpu.SMEM((1,), F32),
         pltpu.SMEM((4,), jnp.int32),
-        pltpu.VMEM((3, OWN, HID), F32),
         pltpu.VMEM((4, 2, 2 * ROWS, WIDTH), BF16),
-        pltpu.VMEM((4 * WIDTH, HID), BF16),
-        pltpu.VMEM((4 * WIDTH, HID), BF16),
-        pltpu.VMEM((4 * WIDTH, HID), BF16),
+        pltpu.VMEM((3, 4 * WIDTH, HID), BF16),
         pltpu.VMEM((2 * ROWS, HID), F32),
         pltpu.VMEM((2 * ROWS, HID), F32),
         pltpu.VMEM((2 * ROWS, HID), F32),
@@ -358,7 +355,7 @@
     scratch += first + first + second + second
     scratch += [pltpu.VMEM((SIZE[c], OWN, w), F32) for a, c, _, w, _, _ in STREAMS]
     dma = pltpu.SemaphoreType.DMA
-    scratch += [dma((8,)), dma((6,)), dma((6,)), dma((8,)), dma((8,)), dma((5,)), dma((5,)), dma((n,))]
+    scratch += [dma((6,)), dma((2,)), dma((6,)), dma((8,)), dma((5,)), dma((5,))]
     scratch += [dma((2 * n,)), dma((counts()[1],))]
     hbm = pl.BlockSpec(memory_space=pl.ANY)
     result = pl.pallas_call(

time: 55.2 us -> 54.7 us (level)
  no operation moved by 1% of the time
where the time goes in v5:
time: 54.7 us; the launch traced here: 54.6 us
  Pallas kernels  53.2 us (97%)
  local copies, waits for them, and re-layouts  0.7 us (1%)
  between operations  0.66 us (1%)
    pallas_call x1, Pallas kernels, shards(): pl.pallas_call(kernel, out_shape=pltpu.VMEM((3, OWN, HID), F32), in_specs...  53.2 us

profile of v5, /device:TPU:8, one launch (start us, length us, event | category | flops | bytes accessed | tf_op | source)
XLA Modules:
  0.0 54.6 jit_solution(390963965030967180)
XLA Ops:
  0.7 53.2 %shard_map.82 = f32[3,32,640]{2,1,0:T(8,128)S(1)} custom-call(bf16[128,512]{1,0:T(8,128)(2,1)} %tok.1, bf16[128,512]{1,0:T(8,128)(2,1)} %gout.1, bf16[2048,640]{1,0:T(8,128)(2,1)} %w_gate.1, bf16[2048,640]{1,0:T(8,128)(2,1)} %w_lin.1, bf16[2048,640]{1,0:T(8,128)(2,1)} %w_out.1, f32[1,5]{1,0:T(1,128)} %code.1, f32[1]{0:T(128)S(6)} %copy.11.decode, s32[4]{0:T(128)} %strag.1), custom_call_target="tpu_custom_call" | custom-call | tf_op jit(solution)/shard_map/pallas_call | solution.py:361
  53.9 0.7 %copy.10 = f32[32,3,640]{2,0,1:T(8,128)} copy(f32[32,3,640]{2,0,1:T(8,128)S(1)} %bitcast.1) | data formatting | bytes 491520

commit v6 on v5

--- a/solution.py
+++ b/solution.py
@@ -20,23 +20,21 @@
 LANES = 128
 
 STREAMS = (
-    ("y", "z", 1280, 128, -1, 1),
-    ("y", "z", 0, 128, 1, 1),
-    ("y", "z", 1408, 128, 1, 0),
-    ("z", "y", 1536, 128, -1, 0),
-    ("z", "y", 1664, 256, -1, 0),
-    ("y", "z", 640, 128, -1, 1),
-    ("z", "y", 768, 256, 1, 0),
-    ("y", "z", 384, 256, -1, 1),
-    ("y", "z", 1024, 256, 1, 1),
-    ("z", "y", 128, 256, 1, 0),
+    ("y", "z", 1792, 128, 1, 1),
+    ("z", "y", 1536, 128, 1, 1),
+    ("z", "y", 1280, 256, -1, 0),
+    ("z", "y", 1664, 128, 1, 0),
+    ("y", "z", 1024, 256, -1, 1),
+    ("y", "z", 0, 384, 1, 1),
+    ("z", "y", 896, 128, 1, 1),
+    ("z", "y", 384, 256, -1, 1),
+    ("y", "z", 640, 256, -1, 1),
 )
 ORDER = (
-    2, 2, 2, 3, 3, 3, 9, 9, 9, 8, 8, 8, 4, 4, 4, 6, 6, 6, 0, 0, 0, 5, 5, 5, 7, 3, 3, 7, 1, 2,
-    1, 7, 1, 9, 9, 4, 4, 8, 6, 6, 3, 3, 0, 9, 9, 5, 4, 4, 2, 2, 2, 6, 6, 7, 1, 3, 9, 0, 0, 0,
-    0, 0, 4, 2, 2, 5, 5, 5, 5, 5, 6, 8, 8, 8, 8, 8, 3, 3, 3, 9, 9, 9, 1, 1, 7, 7, 7, 7, 0, 1,
-    1, 7, 1, 0, 2, 0, 4, 4, 4, 2, 3, 5, 9, 6, 6, 6, 5, 5, 8, 4, 8, 3, 8, 7, 1, 7, 9, 7, 6, 1,
-    1, 2, 0, 4, 5, 8, 6, 7, 1, 2,
+    7, 7, 7, 3, 3, 0, 0, 3, 0, 4, 4, 4, 1, 1, 1, 2, 2, 2, 6, 6, 6, 5, 5, 8, 8, 5, 8, 7, 7, 0,
+    3, 3, 1, 1, 2, 2, 4, 6, 6, 7, 7, 3, 3, 8, 1, 1, 5, 2, 2, 6, 6, 7, 3, 0, 0, 0, 0, 0, 1, 4,
+    4, 4, 4, 4, 2, 6, 3, 3, 3, 7, 7, 7, 7, 5, 5, 8, 8, 8, 8, 5, 5, 8, 5, 0, 0, 1, 1, 1, 0, 1,
+    4, 3, 4, 4, 6, 6, 6, 6, 2, 2, 2, 7, 5, 1, 8, 3, 8, 8, 5, 5, 2, 6, 0, 4, 8, 2, 5,
 )
 BLOCKS = ((0, 128), (128, 384), (384, 640))
 
@@ -131,7 +129,7 @@
     barrier = pltpu.get_barrier_semaphore()
     partners = [right, left, sibling]
     partners += [ring_device(axis, d) for axis in ("y", "z") for d in (1, -1)]
-    partners += [ring_device(axis, d) for axis in ("z",) for d in (2, -2)]
+    partners += [ring_device(axis, d) for axis in ("y", "z",) for d in (2, -2)]
     for partner in partners:
         pl.semaphore_signal(barrier, inc=1, device_id=partner, device_id_type=MESH)
 
@@ -242,16 +240,17 @@
         other = jnp.where(y == 0, 1 - a, a)
         for j in (1, 2, 3, 4):
             total = total + jnp.where(z >= j, tab[j, a, j : j + 1, :], ytab[j - 1, other, j : j + 1, :])
-        weight.append(jnp.concatenate([total, total], axis=1))
+        weight.append(jnp.concatenate([total] * 4, axis=1))
 
     finished = set()
 
     def finish(block):
         lower, upper = BLOCKS[block]
+        chunk = 16384 // (upper - lower)
         forward(2 * (1 - x_hi) + 1 - core, False, lower, upper)
 
         def elementwise(i, carry):
-            rows = pl.ds(pl.multiple_of(i * 32, 32), 32)
+            rows = pl.ds(pl.multiple_of(i * chunk, chunk), chunk)
             act, slope = gelu_parts(acc_g[rows, lower:upper])
             lin, dh = acc_l[rows, lower:upper], acc_h[rows, lower:upper]
             dmat[rows, lower:upper] = (dh * lin * slope).astype(BF16)
@@ -259,7 +258,7 @@
             dmat[rows, 2 * HID + lower : 2 * HID + upper] = (act * lin).astype(BF16)
             return carry
 
-        lax.fori_loop(0, 2 * ROWS // 32, elementwise, 0)
+        lax.fori_loop(0, 2 * ROWS // chunk, elementwise, 0)
 
     def products(s):
         col, width = STREAMS[s][2:4]

time: 54.7 us -> 54.6 us (level); the launches traced: 54.6 us -> 53.9 us
  Pallas kernels: 53.2 us -> 52.6 us
    pallas_call x1, Pallas kernels: 53.2 us -> 52.6 us  [shards(): pl.pallas_call(kernel, out_shape=pltpu.VMEM((3, OWN, HID), F32), in_specs...]
where the time goes in v6:
time: 54.6 us; the launch traced here: 53.9 us
  Pallas kernels  52.6 us (96%)
  local copies, waits for them, and re-layouts  0.7 us (1%)
  between operations  0.66 us (1%)
    pallas_call x1, Pallas kernels, shards(): pl.pallas_call(kernel, out_shape=pltpu.VMEM((3, OWN, HID), F32), in_specs...  52.6 us

profile of v6, /device:TPU:8, one launch (start us, length us, event | category | flops | bytes accessed | tf_op | source)
XLA Modules:
  0.0 53.9 jit_solution(11028809599055188858)
XLA Ops:
  0.7 52.6 %shard_map.82 = f32[3,32,640]{2,1,0:T(8,128)S(1)} custom-call(bf16[128,512]{1,0:T(8,128)(2,1)} %tok.1, bf16[128,512]{1,0:T(8,128)(2,1)} %gout.1, bf16[2048,640]{1,0:T(8,128)(2,1)} %w_gate.1, bf16[2048,640]{1,0:T(8,128)(2,1)} %w_lin.1, bf16[2048,640]{1,0:T(8,128)(2,1)} %w_out.1, f32[1,5]{1,0:T(1,128)} %code.1, f32[1]{0:T(128)S(6)} %copy.11.decode, s32[4]{0:T(128)} %strag.1), custom_call_target="tpu_custom_call" | custom-call | tf_op jit(solution)/shard_map/pallas_call | solution.py:360
  53.2 0.7 %copy.10 = f32[32,3,640]{2,0,1:T(8,128)} copy(f32[32,3,640]{2,0,1:T(8,128)S(1)} %bitcast.1) | data formatting | bytes 491520
